TPU v7x, 32 devices: a whole 2x2x4 slice. The times are simulated.
32 devices in a mesh: dp: 2 (over y), expert: 8 (over z, x), etp: 2 (over core).
Axes of the slice: x: 2, y: 2, z: 4, core: 2. Of those that a mesh axis runs over, the one named last changes fastest.
Arguments:
- tokens: bfloat16 [1024, 4096], P(('dp', 'expert'), 'etp'), may hold values from -6 to 6
- expert_ids: int32 [1024, 8], P(('dp', 'expert')), may hold values from 0 to 15, all different within a row; in each aligned block of 64 rows (0 to 63, 64 to 127, ...) at most 48 rows name the same one
- combine: float32 [1024, 8], P(('dp', 'expert')), may hold values from 0.05 to 1
- gate_weight: bfloat16 [16, 4096, 1536], P('expert', 'dp', 'etp'), may hold values from -0.09375 to 0.09375
- up_weight: bfloat16 [16, 4096, 1536], P('expert', 'dp', 'etp'), may hold values from -0.09375 to 0.09375
- down_weight: bfloat16 [16, 1536, 4096], P('expert', 'etp', 'dp'), may hold values from -0.15625 to 0.15625
Outputs:
- mixed: bfloat16 [1024, 4096], P(('dp', 'expert'), 'etp')
Inputs may be any that keep to these rules, and one draw needn't show every extreme that they name: `expert_ids`: each row names 8 different experts. In the rows of one device (aligned blocks of 64 rows) no expert is named by more than 48 rows, a bound that some block reaches.
All inputs are finite; a program needn't handle non-finite values.
Results may differ from a plain program's by a relative error of at most 0.008.
Values may be sent and summed in bfloat16 or wider, within the bound.
A program may use at most 192 MiB of HBM per device.

v0:
```python
import jax
import jax.numpy as jnp
from jax import lax
from jax.sharding import PartitionSpec as P


def ring_steps(columns):
    ring = list(range(0, columns, 2)) + list(range(1, columns, 2))[::-1]
    ahead = [(ring[i], ring[(i + 1) % columns]) for i in range(columns)]
    return ahead, [(b, a) for a, b in ahead]


def ring_spread(block, groups, columns, cores):
    perm = [
        (((d - c) % groups) * cores + d, d * cores + c) for d in range(groups) for c in range(cores)
    ]
    ahead, back = ring_steps(columns)
    block = lax.ppermute(block, ("dp", "etp"), perm)
    held = {0: block}
    up = down = block
    for step in range(1, columns // 2 + 1):
        up = lax.ppermute(up, "expert", ahead)
        held[step] = up
        if columns - step > step:
            down = lax.ppermute(down, "expert", back)
            held[columns - step] = down
    swap = [(0, 1), (1, 0)]
    other = {k: lax.ppermute(held[k], "etp", swap) for k in held}
    first = lax.axis_index("etp") == 0
    pairs = [(held[k], other[k]) for k in range(columns)]
    return (
        jnp.stack([jnp.where(first, a, b) for a, b in pairs]),
        jnp.stack([jnp.where(first, b, a) for a, b in pairs]),
    )


def ring_collect(parts, groups, columns, cores):
    ahead, back = ring_steps(columns)
    first = lax.axis_index("etp") == 0
    mine = jnp.where(first, parts[0], parts[1])
    away = jnp.where(first, parts[1], parts[0])
    half = mine.shape[1] // 2
    order = [k for s in range(1, columns // 2 + 1) for k in (s, columns - s)] + [0]
    other = {}
    for k in order:
        if k not in other:
            other[k] = lax.ppermute(away[k], "etp", [(0, 1), (1, 0)])

    def own(k, low):
        rows = slice(0, half) if low else slice(half, None)
        return mine[k, rows].astype(jnp.float32) + other[k][rows].astype(jnp.float32)

    up = own(1, True).astype(jnp.bfloat16)
    down = own(columns - 1, False).astype(jnp.bfloat16)
    for step in range(2, columns + 1):
        up = lax.ppermute(up, "expert", ahead)
        down = lax.ppermute(down, "expert", back)
        up = (up.astype(jnp.float32) + own(step % columns, True)).astype(jnp.bfloat16)
        down = (down.astype(jnp.float32) + own(columns - step, False)).astype(jnp.bfloat16)
    perm = [
        (d * cores + c, ((d - c) % groups) * cores + d) for d in range(groups) for c in range(cores)
    ]
    return lax.ppermute(jnp.concatenate([up, down]), ("dp", "etp"), perm)


def spread_tokens(tokens, groups, cores, width):
    rows = tokens.shape[0]
    if groups == cores:
        perm = [
            (((d - c) % groups) * cores + d, d * cores + c)
            for d in range(groups)
            for c in range(cores)
        ]
        swapped = lax.ppermute(tokens, ("dp", "etp"), perm)
        along = lax.all_gather(swapped, "expert", axis=0)
        return lax.all_gather(along, "etp", axis=0)
    full = lax.all_gather(tokens, "etp", axis=1, tiled=True)
    mine = lax.all_to_all(
        full.reshape(rows, groups, width), "dp", split_axis=1, concat_axis=0, tiled=False
    )
    mine = mine.reshape(groups, rows, width)
    order = jnp.mod(lax.axis_index("dp") - jnp.arange(groups), groups)
    return lax.all_gather(jnp.take(mine, order, axis=0), "expert", axis=1)


def collect_output(parts, groups, cores, width):
    stacked = jnp.stack(parts)
    if groups == cores:
        summed = lax.psum_scatter(stacked, "etp", scatter_dimension=0, tiled=False)
        summed = lax.psum_scatter(summed, "expert", scatter_dimension=0, tiled=False)
        perm = [
            (d * cores + c, ((d - c) % groups) * cores + d)
            for d in range(groups)
            for c in range(cores)
        ]
        return lax.ppermute(summed, ("dp", "etp"), perm)
    summed = lax.psum_scatter(stacked, "expert", scatter_dimension=1, tiled=False)
    order = jnp.mod(lax.axis_index("dp") - jnp.arange(groups), groups)
    summed = lax.psum(jnp.take(summed, order, axis=0).astype(jnp.float32), "etp")
    back = lax.all_to_all(
        summed.astype(jnp.bfloat16), "dp", split_axis=0, concat_axis=1, tiled=True
    )
    back = back.reshape(back.shape[1] // groups, -1) if back.ndim == 2 else back
    rows = back.shape[-2] // groups
    back = back.reshape(groups, rows, width).transpose(1, 0, 2).reshape(rows, cores, -1)
    return lax.dynamic_index_in_dim(back, lax.axis_index("etp"), 1, keepdims=False)


def shards(tokens, expert_ids, combine, gate_weight, up_weight, down_weight):
    rows, top_count = expert_ids.shape
    held, width, _ = gate_weight.shape
    groups = lax.axis_size("dp")
    columns = lax.axis_size("expert")
    cores = lax.axis_size("etp")
    experts = held * columns
    capacity = min(rows, 3 * rows * top_count // (2 * experts))
    group = lax.axis_index("dp")

    named = expert_ids[:, :, None] == jnp.arange(experts, dtype=jnp.int32)[None, None, :]
    weight = jnp.sum(jnp.where(named, combine[:, :, None], 0.0), axis=1)
    near = groups == cores == 2 and columns % 2 == 0
    if near:
        high = weight.T.astype(jnp.bfloat16)
        low = (weight.T - high.astype(jnp.float32)).astype(jnp.bfloat16)
        extra = jnp.stack([high, low]).reshape(-1)
        extra_rows = -(-extra.size // (8 * tokens.shape[1])) * 8
        extra = jnp.pad(extra, (0, extra_rows * tokens.shape[1] - extra.size))
        block = jnp.concatenate([tokens, extra.reshape(extra_rows, -1)])
        whole = ring_spread(block, groups, columns, cores)
        spread = [a[:, :rows] for a in whole]
        tail = jnp.stack([a[:, rows:] for a in whole]).reshape(groups * columns, -1)
        tail = tail[:, : 2 * experts * rows].reshape(-1, 2, experts, rows).astype(jnp.float32)
        weight = tail[:, 0] + tail[:, 1]
    else:
        spread = spread_tokens(tokens, groups, cores, width)
        weight = lax.all_gather(weight.T, ("dp", "expert"), axis=0)
    weight = lax.dynamic_slice_in_dim(weight, lax.axis_index("expert") * held, held, axis=1)
    chosen = (weight > 0).astype(jnp.bfloat16)
    earlier = jnp.triu(jnp.ones((rows, rows), jnp.bfloat16), 1)
    place = jnp.einsum("bet,tu->beu", chosen, earlier, preferred_element_type=jnp.float32)
    slots = jnp.arange(capacity, dtype=jnp.float32)[None, None, :, None]
    hit = (place[:, :, None, :] == slots) & (weight > 0)[:, :, None, :]
    picker = hit.astype(jnp.bfloat16).reshape(groups, columns, held, capacity, rows)
    slot_weight = jnp.sum(jnp.where(hit, weight[:, :, None, :], 0.0), axis=-1)
    slot_weight = slot_weight.reshape(groups, columns, held, capacity)

    def pick(r):
        which = r if near else jnp.mod(group - r, groups)
        return lax.dynamic_index_in_dim(picker, which, 0, keepdims=False)

    def gate_up(r):
        packed = jnp.einsum(
            "xest,xtk->exsk", pick(r), spread[r], preferred_element_type=jnp.float32
        )
        packed = packed.astype(jnp.bfloat16).reshape(held, columns * capacity, width)
        found = []
        for e in range(held):
            found.append(
                tuple(
                    jnp.dot(packed[e], w[e], preferred_element_type=jnp.float32)
                    for w in (gate_weight, up_weight)
                )
            )
        return found

    gates = [[] for _ in range(held)]
    ups = [[] for _ in range(held)]
    for r in range(1, groups):
        perm = [(d, (d - r) % groups) for d in range(groups)]
        for e, (g, u) in enumerate(gate_up(r)):
            sent = lax.ppermute(
                jnp.concatenate([g, u], axis=1).astype(jnp.bfloat16), "dp", perm
            )
            half = sent.shape[1] // 2
            gates[e].append(sent[:, :half].astype(jnp.float32))
            ups[e].append(sent[:, half:].astype(jnp.float32))
    own_weight = lax.dynamic_index_in_dim(slot_weight, 0 if near else group, 0, keepdims=False)
    own_weight = own_weight.transpose(1, 0, 2).reshape(held, columns * capacity, 1)
    hidden = [[] for _ in range(groups)]
    for e, (g, u) in enumerate(gate_up(0)):
        g = sum(gates[e], g)
        u = sum(ups[e], u)
        h = (jax.nn.silu(g) * u * own_weight[e]).astype(jnp.bfloat16)
        hidden[0].append(h)
        for r in range(1, groups):
            perm = [(d, (d + r) % groups) for d in range(groups)]
            hidden[r].append(lax.ppermute(h, "dp", perm))

    parts = []
    for r in range(groups):
        h = jnp.stack(hidden[r]).reshape(held, columns, capacity, -1)
        dense = jnp.einsum("xest,exsf->xtef", pick(r), h, preferred_element_type=jnp.float32)
        dense = dense.astype(jnp.bfloat16).reshape(columns * rows, -1)
        out = jnp.dot(
            dense, down_weight.reshape(-1, width), preferred_element_type=jnp.float32
        )
        parts.append(out.astype(jnp.bfloat16).reshape(columns, rows, width))
    if near:
        return ring_collect(parts, groups, columns, cores)
    return collect_output(parts, groups, cores, width)


def solution(mesh):
    placed = (
        P(("dp", "expert"), "etp"),
        P(("dp", "expert"), None),
        P(("dp", "expert"), None),
        P("expert", "dp", "etp"),
        P("expert", "dp", "etp"),
        P("expert", "etp", "dp"),
    )
    return jax.shard_map(
        shards, mesh=mesh, in_specs=placed, out_specs=P(("dp", "expert"), "etp"), check_vma=False
    )
```

profile of v0, /device:TPU:1, one launch (start us, length us, event | category | flops | bytes accessed | tf_op | source)
XLA Modules:
  0.0 231.4 jit_solution(8014396012982907440)
XLA Ops:
  1.9 4.0 %collective-permute-start = (bf16[72,2048]{1,0:T(8,128)(2,1)S(1)}, bf16[72,2048]{1,0:T(8,128)(2,1)S(1)}, u32[]{:S(2)}, u32[]{:S(2)}) collective-permute-start(bf16[72,2048]{1,0:T(8,128)(2,1)S(1)} %pad_maximum_fusion.2), channel_id=1, source_target_pairs={{0,0},{16,1},{17,16},{1,17},{2,2},{18,3},{19,18},{3,19},{4,4},{20,... | collective-permute-start | bytes 884744 | tf_op jit(solution)/shard_map/ppermute | solution.py:18
  5.8 5.2 %collective-permute-done = bf16[72,2048]{1,0:T(8,128)(2,1)S(1)} collective-permute-done((bf16[72,2048]{1,0:T(8,128)(2,1)S(1)}, bf16[72,2048]{1,0:T(8,128)(2,1)S(1)}, u32[]{:S(2)}, u32[]{:S(2)}) %collective-permute-start) | collective-permute-done | bytes 294944 | tf_op jit(solution)/shard_map/ppermute | solution.py:18
  12.5 4.1 %collective-permute-done.2 = bf16[72,2048]{1,0:T(8,128)(2,1)S(1)} collective-permute-done((bf16[72,2048]{1,0:T(8,128)(2,1)S(1)}, bf16[72,2048]{1,0:T(8,128)(2,1)S(1)}, u32[]{:S(2)}, u32[]{:S(2)}) %collective-permute-start.2) | collective-permute-done | bytes 294944 | tf_op jit(solution)/shard_map/ppermute | solution.py:22
  19.3 5.4 %collective-permute-done.4 = bf16[72,2048]{1,0:T(8,128)(2,1)S(1)} collective-permute-done((bf16[72,2048]{1,0:T(8,128)(2,1)S(1)}, bf16[72,2048]{1,0:T(8,128)(2,1)S(1)}, u32[]{:S(2)}, u32[]{:S(2)}) %collective-permute-start.4) | collective-permute-done | bytes 294944 | tf_op jit(solution)/shard_map/ppermute | solution.py:22
  24.7 1.4 collective-permute-start.5
  28.2 6.4 %collective-permute-done.6 = bf16[72,2048]{1,0:T(8,128)(2,1)S(1)} collective-permute-done((bf16[72,2048]{1,0:T(8,128)(2,1)S(1)}, bf16[72,2048]{1,0:T(8,128)(2,1)S(1)}, u32[]{:S(2)}, u32[]{:S(2)}) %collective-permute-start.6) | collective-permute-done | bytes 294944 | tf_op jit(solution)/shard_map/ppermute | solution.py:22
  37.2 6.9 %collective-permute-done.8 = bf16[72,2048]{1,0:T(8,128)(2,1)S(1)} collective-permute-done((bf16[72,2048]{1,0:T(8,128)(2,1)S(1)}, bf16[72,2048]{1,0:T(8,128)(2,1)S(1)}, u32[]{:S(2)}, u32[]{:S(2)}) %collective-permute-start.8) | collective-permute-done | bytes 294944 | tf_op jit(solution)/shard_map/ppermute | solution.py:22
  46.6 1.4 copy-done
  52.7 1.4 fusion.28
  54.6 1.4 fusion.31
  56.1 1.4 fusion.34
  57.5 1.4 fusion.37
  60.0 3.8 %collective-permute-start.16 = (bf16[384,1536]{1,0:T(8,128)(2,1)}, bf16[384,1536]{1,0:T(8,128)(2,1)}, u32[]{:S(2)}, u32[]{:S(2)}) collective-permute-start(bf16[384,1536]{1,0:T(8,128)(2,1)} %pad_maximum_fusion), channel_id=1, source_target_pairs={{0,16},{16,0},{1,17},{17,1},{2,18},{18,2},{3,19},{19,3},{4,20},{20... | collective-permute-start | bytes 3538952 | tf_op jit(solution)/shard_map/ppermute | solution.py:171
  65.5 2.5 %fusion.14 = f32[384,768]{1,0:T(8,128)} fusion(bf16[384,2048]{1,0:T(8,128)(2,1)S(1)} %bitcast.265, bf16[2,2048,768]{2,1,0:T(8,128)(2,1)S(1)} %bitcast.275), kind=kOutput, calls=%fused_computation.16 | convolution fusion | flops 1207959552 | bytes 5898240 | tf_op jit(solution)/shard_map/dot_general | solution.py:160
  68.2 3.4 %fusion.6 = f32[384,768]{1,0:T(8,128)S(1)} fusion(bf16[384,2048]{1,0:T(8,128)(2,1)S(1)} %bitcast.263, bf16[2,2048,768]{2,1,0:T(8,128)(2,1)} %param.9), kind=kOutput, calls=%fused_computation.8 | convolution fusion | flops 1207959552 | bytes 5898240 | tf_op jit(solution)/shard_map/dot_general | solution.py:160
  71.7 18.4 %collective-permute-done.16 = bf16[384,1536]{1,0:T(8,128)(2,1)} collective-permute-done((bf16[384,1536]{1,0:T(8,128)(2,1)}, bf16[384,1536]{1,0:T(8,128)(2,1)}, u32[]{:S(2)}, u32[]{:S(2)}) %collective-permute-start.16) | collective-permute-done | bytes 1179680 | tf_op jit(solution)/shard_map/ppermute | solution.py:171
  90.1 3.9 %multiply_convert_fusion.1 = bf16[384,768]{1,0:T(8,128)(2,1)S(1)} fusion(f32[384,768]{1,0:T(8,128)S(1)} %copy-done.2, bf16[384,1536]{1,0:T(8,128)(2,1)} %collective-permute-done.16, f32[384]{0:T(512)S(1)} %mul.39, bf16[384,2048]{1,0:T(8,128)(2,1)S(1)} %bitcast.266, bf16[2,2048,768]{2,1,0:T(8,128)(2,1)} %param.10), kind=kOutput, calls=%fused_computation.51 | convolution fusion | flops 1211203584 | bytes 7669248 | tf_op jit(solution)/shard_map/dot_general | solution.py:160
  95.3 20.1 %collective-permute-done.17 = bf16[384,1536]{1,0:T(8,128)(2,1)} collective-permute-done((bf16[384,1536]{1,0:T(8,128)(2,1)}, bf16[384,1536]{1,0:T(8,128)(2,1)}, u32[]{:S(2)}, u32[]{:S(2)}) %collective-permute-start.17) | collective-permute-done | bytes 1179680 | tf_op jit(solution)/shard_map/ppermute | solution.py:171
  115.4 2.8 %multiply_convert_fusion = bf16[384,768]{1,0:T(8,128)(2,1)S(1)} fusion(f32[384,768]{1,0:T(8,128)S(1)} %fusion.6, bf16[384,1536]{1,0:T(8,128)(2,1)} %collective-permute-done.17, f32[384]{0:T(512)S(1)} %mul.44, bf16[384,2048]{1,0:T(8,128)(2,1)S(1)} %bitcast.264, bf16[2,2048,768]{2,1,0:T(8,128)(2,1)S(1)} %bitcast.279), kind=kOutput, calls=%fused_computation.50 | convolution fusion | flops 1211203584 | bytes 7669760 | tf_op jit(solution)/shard_map/dot_general | solution.py:160
  120.1 1.6 copy.40
  122.0 5.9 %collective-permute-done.18 = bf16[384,768]{1,0:T(8,128)(2,1)S(1)} collective-permute-done((bf16[384,768]{1,0:T(8,128)(2,1)S(1)}, bf16[384,768]{1,0:T(8,128)(2,1)S(1)}, u32[]{:S(2)}, u32[]{:S(2)}) %collective-permute-start.18) | collective-permute-done | bytes 589856 | tf_op jit(solution)/shard_map/ppermute | solution.py:187
  127.9 12.6 %collective-permute-done.19 = bf16[384,768]{1,0:T(8,128)(2,1)S(1)} collective-permute-done((bf16[384,768]{1,0:T(8,128)(2,1)S(1)}, bf16[384,768]{1,0:T(8,128)(2,1)S(1)}, u32[]{:S(2)}, u32[]{:S(2)}) %collective-permute-start.19) | collective-permute-done | bytes 589856 | tf_op jit(solution)/shard_map/ppermute | solution.py:187
  141.2 1.6 copy.43
  143.1 3.7 %convolution_convert_fusion.2 = bf16[512,2048]{1,0:T(8,128)(2,1)S(1)} fusion(bf16[512,1536]{1,0:T(8,128)(2,1)S(1)} %bitcast.262, bf16[1536,2048]{1,0:T(8,128)(2,1)S(1)} %bitcast.282), kind=kOutput, calls=%fused_computation.20 | convolution fusion | flops 3222274048 | bytes 9961472 | tf_op jit(solution)/shard_map/dot_general | solution.py:194
  146.8 3.6 %broadcast_select_fusion.1 = (bf16[512,2048]{1,0:T(8,128)(2,1)S(1)}, bf16[512,2048]{1,0:T(8,128)(2,1)S(1)}) fusion(bf16[512,2048]{1,0:T(8,128)(2,1)S(1)} %convolution_convert_fusion.2, pred[]{:T(512)S(6)} %eq.39, bf16[512,1536]{1,0:T(8,128)(2,1)S(1)} %bitcast.261, bf16[1536,2048]{1,0:T(8,128)(2,1)S(1)} %bitcast.283), kind=kOutput, calls=%fused_computation.33 | convolution fusion | flops 3224371200 | bytes 14155777 | tf_op jit(solution)/shard_map/dot_general | solution.py:194
  155.0 2.7 %collective-permute-done.21 = bf16[32,2048]{1,0:T(8,128)(2,1)S(1)} collective-permute-done((bf16[32,2048]{1,0:T(8,128)(2,1)S(1)}, bf16[32,2048]{1,0:T(8,128)(2,1)S(1)}, u32[]{:S(2)}, u32[]{:S(2)}) %collective-permute-start.21) | collective-permute-done | bytes 131104 | tf_op jit(solution)/shard_map/ppermute | solution.py:56
  157.7 1.4 collective-permute-start.23
  159.1 1.5 collective-permute-start.26
  161.7 1.4 collective-permute-start.25
  163.0 2.7 %collective-permute-start.28 = (bf16[64,2048]{1,0:T(8,128)(2,1)S(1)}, bf16[64,2048]{1,0:T(8,128)(2,1)S(1)}, u32[]{:S(2)}, u32[]{:S(2)}) collective-permute-start(bf16[64,2048]{1,0:T(8,128)(2,1)S(1)} %get-tuple-element.20), channel_id=1, source_target_pairs={{0,1},{1,0},{2,3},{3,2},{4,5},{5,4},{6,7},{7,6},{8,9},{9,8},{10,11... | collective-permute-start | bytes 786440 | tf_op jit(solution)/shard_map/ppermute | solution.py:47
  167.1 3.9 %collective-permute-start.30 = (bf16[64,2048]{1,0:T(8,128)(2,1)S(1)}, bf16[64,2048]{1,0:T(8,128)(2,1)S(1)}, u32[]{:S(2)}, u32[]{:S(2)}) collective-permute-start(bf16[64,2048]{1,0:T(8,128)(2,1)S(1)} %get-tuple-element.19), channel_id=1, source_target_pairs={{0,1},{1,0},{2,3},{3,2},{4,5},{5,4},{6,7},{7,6},{8,9},{9,8},{10,11... | collective-permute-start | bytes 786440 | tf_op jit(solution)/shard_map/ppermute | solution.py:47
  172.3 3.9 %collective-permute-start.32 = (bf16[64,2048]{1,0:T(8,128)(2,1)S(1)}, bf16[64,2048]{1,0:T(8,128)(2,1)S(1)}, u32[]{:S(2)}, u32[]{:S(2)}) collective-permute-start(bf16[64,2048]{1,0:T(8,128)(2,1)S(1)} %get-tuple-element.18), channel_id=1, source_target_pairs={{0,1},{1,0},{2,3},{3,2},{4,5},{5,4},{6,7},{7,6},{8,9},{9,8},{10,11... | collective-permute-start | bytes 786440 | tf_op jit(solution)/shard_map/ppermute | solution.py:47
  177.5 3.6 %collective-permute-done.31 = bf16[32,2048]{1,0:T(8,128)(2,1)S(1)} collective-permute-done((bf16[32,2048]{1,0:T(8,128)(2,1)S(1)}, bf16[32,2048]{1,0:T(8,128)(2,1)S(1)}, u32[]{:S(2)}, u32[]{:S(2)}) %collective-permute-start.31) | collective-permute-done | bytes 131104 | tf_op jit(solution)/shard_map/ppermute | solution.py:56
  181.2 2.0 collective-permute-start.35
  183.2 2.2 collective-permute-done.35
  185.4 2.0 collective-permute-start.36
  187.4 1.9 collective-permute-done.36
  189.4 1.9 collective-permute-start.37
  191.3 2.5 %collective-permute-done.37 = bf16[32,2048]{1,0:T(8,128)(2,1)S(1)} collective-permute-done((bf16[32,2048]{1,0:T(8,128)(2,1)S(1)}, bf16[32,2048]{1,0:T(8,128)(2,1)S(1)}, u32[]{:S(2)}, u32[]{:S(2)}) %collective-permute-start.37) | collective-permute-done | bytes 131104 | tf_op jit(solution)/shard_map/ppermute | solution.py:57
  193.9 1.4 collective-permute-start.38
  195.2 3.2 %collective-permute-done.38 = bf16[32,2048]{1,0:T(8,128)(2,1)S(1)} collective-permute-done((bf16[32,2048]{1,0:T(8,128)(2,1)S(1)}, bf16[32,2048]{1,0:T(8,128)(2,1)S(1)}, u32[]{:S(2)}, u32[]{:S(2)}) %collective-permute-start.38) | collective-permute-done | bytes 131104 | tf_op jit(solution)/shard_map/ppermute | solution.py:57
  199.6 3.2 %collective-permute-done.39 = bf16[32,2048]{1,0:T(8,128)(2,1)S(1)} collective-permute-done((bf16[32,2048]{1,0:T(8,128)(2,1)S(1)}, bf16[32,2048]{1,0:T(8,128)(2,1)S(1)}, u32[]{:S(2)}, u32[]{:S(2)}) %collective-permute-start.39) | collective-permute-done | bytes 131104 | tf_op jit(solution)/shard_map/ppermute | solution.py:57
  202.8 2.2 collective-permute-start.40
  205.0 11.4 %collective-permute-start.34 = (bf16[64,2048]{1,0:T(8,128)(2,1)S(1)}, bf16[64,2048]{1,0:T(8,128)(2,1)S(1)}, u32[]{:S(2)}, u32[]{:S(2)}) collective-permute-start(bf16[64,2048]{1,0:T(8,128)(2,1)S(1)} %get-tuple-element.17), channel_id=1, source_target_pairs={{0,1},{1,0},{2,3},{3,2},{4,5},{5,4},{6,7},{7,6},{8,9},{9,8},{10,11... | collective-permute-start | bytes 786440 | tf_op jit(solution)/shard_map/ppermute | solution.py:47
  216.5 1.5 collective-permute-start.41
  218.0 3.5 %collective-permute-done.33 = bf16[32,2048]{1,0:T(8,128)(2,1)S(1)} collective-permute-done((bf16[32,2048]{1,0:T(8,128)(2,1)S(1)}, bf16[32,2048]{1,0:T(8,128)(2,1)S(1)}, u32[]{:S(2)}, u32[]{:S(2)}) %collective-permute-start.33) | collective-permute-done | bytes 131104 | tf_op jit(solution)/shard_map/ppermute | solution.py:56
  221.6 5.8 %collective-permute-start.42 = (bf16[64,2048]{1,0:T(8,128)(2,1)S(1)}, bf16[64,2048]{1,0:T(8,128)(2,1)S(1)}, u32[]{:S(2)}, u32[]{:S(2)}) collective-permute-start(bf16[64,2048]{1,0:T(8,128)(2,1)S(1)} %pad_maximum_fusion.3), channel_id=1, source_target_pairs={{0,0},{1,16},{16,17},{17,1},{2,2},{3,18},{18,19},{19,3},{4,4},{5,2... | collective-permute-start | bytes 786440 | tf_op jit(solution)/shard_map/ppermute | solution.py:63
  227.4 3.3 %collective-permute-done.42 = bf16[64,2048]{1,0:T(8,128)(2,1)S(1)} collective-permute-done((bf16[64,2048]{1,0:T(8,128)(2,1)S(1)}, bf16[64,2048]{1,0:T(8,128)(2,1)S(1)}, u32[]{:S(2)}, u32[]{:S(2)}) %collective-permute-start.42) | collective-permute-done | bytes 262176 | tf_op jit(solution)/shard_map/ppermute | solution.py:63
  (141 shorter events, 37.4 us)
Async XLA Ops:
  1.9 9.2 %collective-permute-start = (bf16[72,2048]{1,0:T(8,128)(2,1)S(1)}, bf16[72,2048]{1,0:T(8,128)(2,1)S(1)}, u32[]{:S(2)}, u32[]{:S(2)}) collective-permute-start(bf16[72,2048]{1,0:T(8,128)(2,1)S(1)} %pad_maximum_fusion.2), channel_id=1, source_target_pairs={{0,0},{16,1},{17,16},{1,17},{2,2},{18,3},{19,18},{3,19},{4,4},{20,... | collective-permute-start | bytes 884744 | tf_op jit(solution)/shard_map/ppermute | solution.py:18
  11.1 5.6 %collective-permute-start.2 = (bf16[72,2048]{1,0:T(8,128)(2,1)S(1)}, bf16[72,2048]{1,0:T(8,128)(2,1)S(1)}, u32[]{:S(2)}, u32[]{:S(2)}) collective-permute-start(bf16[72,2048]{1,0:T(8,128)(2,1)S(1)} %collective-permute-done), channel_id=1, source_target_pairs={{0,4},{4,8},{8,12},{12,14},{14,10},{10,6},{6,2},{2,0},{1,5},{5,9},... | collective-permute-start | bytes 884744 | tf_op jit(solution)/shard_map/ppermute | solution.py:22
  12.4 5.6 %collective-permute-start.10 = (bf16[72,2048]{1,0:T(8,128)(2,1)S(1)}, bf16[72,2048]{1,0:T(8,128)(2,1)S(1)}, u32[]{:S(2)}, u32[]{:S(2)}) collective-permute-start(bf16[72,2048]{1,0:T(8,128)(2,1)S(1)} %collective-permute-done), channel_id=1, source_target_pairs={{4,0},{8,4},{12,8},{14,12},{10,14},{6,10},{2,6},{0,2},{5,1},{9,5},... | collective-permute-start | bytes 884744 | tf_op jit(solution)/shard_map/ppermute | solution.py:25
  12.5 6.7 %collective-permute-start.1 = (bf16[72,2048]{1,0:T(8,128)(2,1)S(1)}, bf16[72,2048]{1,0:T(8,128)(2,1)S(1)}, u32[]{:S(2)}, u32[]{:S(2)}) collective-permute-start(bf16[72,2048]{1,0:T(8,128)(2,1)S(1)} %collective-permute-done), channel_id=1, source_target_pairs={{0,1},{1,0},{2,3},{3,2},{4,5},{5,4},{6,7},{7,6},{8,9},{9,8},{10,11... | collective-permute-start | bytes 884744 | tf_op jit(solution)/shard_map/ppermute | solution.py:28
  16.7 10.9 %collective-permute-start.3 = (bf16[72,2048]{1,0:T(8,128)(2,1)S(1)}, bf16[72,2048]{1,0:T(8,128)(2,1)S(1)}, u32[]{:S(2)}, u32[]{:S(2)}) collective-permute-start(bf16[72,2048]{1,0:T(8,128)(2,1)S(1)} %collective-permute-done.2), channel_id=1, source_target_pairs={{0,1},{1,0},{2,3},{3,2},{4,5},{5,4},{6,7},{7,6},{8,9},{9,8},{10,11... | collective-permute-start | bytes 884744 | tf_op jit(solution)/shard_map/ppermute | solution.py:28
  16.7 8.1 %collective-permute-start.4 = (bf16[72,2048]{1,0:T(8,128)(2,1)S(1)}, bf16[72,2048]{1,0:T(8,128)(2,1)S(1)}, u32[]{:S(2)}, u32[]{:S(2)}) collective-permute-start(bf16[72,2048]{1,0:T(8,128)(2,1)S(1)} %collective-permute-done.2), channel_id=1, source_target_pairs={{0,4},{4,8},{8,12},{12,14},{14,10},{10,6},{6,2},{2,0},{1,5},{5,9},... | collective-permute-start | bytes 884744 | tf_op jit(solution)/shard_map/ppermute | solution.py:22
  18.0 9.4 %collective-permute-start.11 = (bf16[72,2048]{1,0:T(8,128)(2,1)S(1)}, bf16[72,2048]{1,0:T(8,128)(2,1)S(1)}, u32[]{:S(2)}, u32[]{:S(2)}) collective-permute-start(bf16[72,2048]{1,0:T(8,128)(2,1)S(1)} %collective-permute-done.10), channel_id=1, source_target_pairs={{4,0},{8,4},{12,8},{14,12},{10,14},{6,10},{2,6},{0,2},{5,1},{9,5},... | collective-permute-start | bytes 884744 | tf_op jit(solution)/shard_map/ppermute | solution.py:25
  18.1 28.4 %collective-permute-start.15 = (bf16[72,2048]{1,0:T(8,128)(2,1)S(1)}, bf16[72,2048]{1,0:T(8,128)(2,1)S(1)}, u32[]{:S(2)}, u32[]{:S(2)}) collective-permute-start(bf16[72,2048]{1,0:T(8,128)(2,1)S(1)} %collective-permute-done.10), channel_id=1, source_target_pairs={{0,1},{1,0},{2,3},{3,2},{4,5},{5,4},{6,7},{7,6},{8,9},{9,8},{10,11... | collective-permute-start | bytes 884744 | tf_op jit(solution)/shard_map/ppermute | solution.py:28
  24.7 10.8 %collective-permute-start.5 = (bf16[72,2048]{1,0:T(8,128)(2,1)S(1)}, bf16[72,2048]{1,0:T(8,128)(2,1)S(1)}, u32[]{:S(2)}, u32[]{:S(2)}) collective-permute-start(bf16[72,2048]{1,0:T(8,128)(2,1)S(1)} %collective-permute-done.4), channel_id=1, source_target_pairs={{0,1},{1,0},{2,3},{3,2},{4,5},{5,4},{6,7},{7,6},{8,9},{9,8},{10,11... | collective-permute-start | bytes 884744 | tf_op jit(solution)/shard_map/ppermute | solution.py:28
  26.1 8.6 %collective-permute-start.6 = (bf16[72,2048]{1,0:T(8,128)(2,1)S(1)}, bf16[72,2048]{1,0:T(8,128)(2,1)S(1)}, u32[]{:S(2)}, u32[]{:S(2)}) collective-permute-start(bf16[72,2048]{1,0:T(8,128)(2,1)S(1)} %collective-permute-done.4), channel_id=1, source_target_pairs={{0,4},{4,8},{8,12},{12,14},{14,10},{10,6},{6,2},{2,0},{1,5},{5,9},... | collective-permute-start | bytes 884744 | tf_op jit(solution)/shard_map/ppermute | solution.py:22
  27.4 9.4 %collective-permute-start.12 = (bf16[72,2048]{1,0:T(8,128)(2,1)S(1)}, bf16[72,2048]{1,0:T(8,128)(2,1)S(1)}, u32[]{:S(2)}, u32[]{:S(2)}) collective-permute-start(bf16[72,2048]{1,0:T(8,128)(2,1)S(1)} %collective-permute-done.11), channel_id=1, source_target_pairs={{4,0},{8,4},{12,8},{14,12},{10,14},{6,10},{2,6},{0,2},{5,1},{9,5},... | collective-permute-start | bytes 884744 | tf_op jit(solution)/shard_map/ppermute | solution.py:25
  27.6 18.8 %collective-permute-start.14 = (bf16[72,2048]{1,0:T(8,128)(2,1)S(1)}, bf16[72,2048]{1,0:T(8,128)(2,1)S(1)}, u32[]{:S(2)}, u32[]{:S(2)}) collective-permute-start(bf16[72,2048]{1,0:T(8,128)(2,1)S(1)} %collective-permute-done.11), channel_id=1, source_target_pairs={{0,1},{1,0},{2,3},{3,2},{4,5},{5,4},{6,7},{7,6},{8,9},{9,8},{10,11... | collective-permute-start | bytes 884744 | tf_op jit(solution)/shard_map/ppermute | solution.py:28
  34.6 10.3 %collective-permute-start.7 = (bf16[72,2048]{1,0:T(8,128)(2,1)S(1)}, bf16[72,2048]{1,0:T(8,128)(2,1)S(1)}, u32[]{:S(2)}, u32[]{:S(2)}) collective-permute-start(bf16[72,2048]{1,0:T(8,128)(2,1)S(1)} %collective-permute-done.6), channel_id=1, source_target_pairs={{0,1},{1,0},{2,3},{3,2},{4,5},{5,4},{6,7},{7,6},{8,9},{9,8},{10,11... | collective-permute-start | bytes 884744 | tf_op jit(solution)/shard_map/ppermute | solution.py:28
  35.5 8.6 %collective-permute-start.8 = (bf16[72,2048]{1,0:T(8,128)(2,1)S(1)}, bf16[72,2048]{1,0:T(8,128)(2,1)S(1)}, u32[]{:S(2)}, u32[]{:S(2)}) collective-permute-start(bf16[72,2048]{1,0:T(8,128)(2,1)S(1)} %collective-permute-done.6), channel_id=1, source_target_pairs={{0,4},{4,8},{8,12},{12,14},{14,10},{10,6},{6,2},{2,0},{1,5},{5,9},... | collective-permute-start | bytes 884744 | tf_op jit(solution)/shard_map/ppermute | solution.py:22
  36.8 9.4 %collective-permute-start.13 = (bf16[72,2048]{1,0:T(8,128)(2,1)S(1)}, bf16[72,2048]{1,0:T(8,128)(2,1)S(1)}, u32[]{:S(2)}, u32[]{:S(2)}) collective-permute-start(bf16[72,2048]{1,0:T(8,128)(2,1)S(1)} %collective-permute-done.12), channel_id=1, source_target_pairs={{0,1},{1,0},{2,3},{3,2},{4,5},{5,4},{6,7},{7,6},{8,9},{9,8},{10,11... | collective-permute-start | bytes 884744 | tf_op jit(solution)/shard_map/ppermute | solution.py:28
  44.1 2.1 collective-permute-start.9
  49.0 3.0 %slice-start = ((s8[6291456]{0:T(1024)(128)(4,1)}), s8[4194304]{0:T(1024)(128)(4,1)S(1)}, s32[]{:S(2)}) async-start(s8[6291456]{0:T(1024)(128)(4,1)} %bitcast.274), calls=%async_computation | async-start | bytes 8388608
  60.0 30.1 %collective-permute-start.16 = (bf16[384,1536]{1,0:T(8,128)(2,1)}, bf16[384,1536]{1,0:T(8,128)(2,1)}, u32[]{:S(2)}, u32[]{:S(2)}) collective-permute-start(bf16[384,1536]{1,0:T(8,128)(2,1)} %pad_maximum_fusion), channel_id=1, source_target_pairs={{0,16},{16,0},{1,17},{17,1},{2,18},{18,2},{3,19},{19,3},{4,20},{20... | collective-permute-start | bytes 3538952 | tf_op jit(solution)/shard_map/ppermute | solution.py:171
  65.2 50.2 %collective-permute-start.17 = (bf16[384,1536]{1,0:T(8,128)(2,1)}, bf16[384,1536]{1,0:T(8,128)(2,1)}, u32[]{:S(2)}, u32[]{:S(2)}) collective-permute-start(bf16[384,1536]{1,0:T(8,128)(2,1)} %pad_maximum_fusion.1), channel_id=1, source_target_pairs={{0,16},{16,0},{1,17},{17,1},{2,18},{18,2},{3,19},{19,3},{4,20},{20... | collective-permute-start | bytes 3538952 | tf_op jit(solution)/shard_map/ppermute | solution.py:171
  68.2 21.9 %copy-start.2 = (f32[384,768]{1,0:T(8,128)S(1)}, f32[384,768]{1,0:T(8,128)}, u32[]{:S(2)}) copy-start(f32[384,768]{1,0:T(8,128)} %fusion.14) | copy-start | bytes 3538948
  68.2 47.2 %slice-start.4 = ((s8[6291456]{0:T(1024)(128)(4,1)}), s8[4194304]{0:T(1024)(128)(4,1)S(1)}, s32[]{:S(2)}) async-start(s8[6291456]{0:T(1024)(128)(4,1)} %bitcast.278), calls=%async_computation.4 | async-start | bytes 8388608
  71.6 43.7 %slice-start.5 = ((s8[6291456]{0:T(1024)(128)(4,1)}), s8[2097152]{0:T(1024)(128)(4,1)S(1)}, s32[]{:S(2)}) async-start(s8[6291456]{0:T(1024)(128)(4,1)} %bitcast.278), calls=%async_computation.5 | async-start | bytes 4194304
  94.0 33.9 %collective-permute-start.18 = (bf16[384,768]{1,0:T(8,128)(2,1)S(1)}, bf16[384,768]{1,0:T(8,128)(2,1)S(1)}, u32[]{:S(2)}, u32[]{:S(2)}) collective-permute-start(bf16[384,768]{1,0:T(8,128)(2,1)S(1)} %multiply_convert_fusion.1), channel_id=1, source_target_pairs={{0,16},{16,0},{1,17},{17,1},{2,18},{18,2},{3,19},{19,3},{4,20},{20... | collective-permute-start | bytes 1769480 | tf_op jit(solution)/shard_map/ppermute | solution.py:187
  118.2 22.3 %collective-permute-start.19 = (bf16[384,768]{1,0:T(8,128)(2,1)S(1)}, bf16[384,768]{1,0:T(8,128)(2,1)S(1)}, u32[]{:S(2)}, u32[]{:S(2)}) collective-permute-start(bf16[384,768]{1,0:T(8,128)(2,1)S(1)} %multiply_convert_fusion), channel_id=1, source_target_pairs={{0,16},{16,0},{1,17},{17,1},{2,18},{18,2},{3,19},{19,3},{4,20},{20... | collective-permute-start | bytes 1769480 | tf_op jit(solution)/shard_map/ppermute | solution.py:187
  120.1 23.0 %slice-start.6 = ((s8[6291456]{0:T(1024)(128)(4,1)}), s8[4194304]{0:T(1024)(128)(4,1)S(1)}, s32[]{:S(2)}) async-start(s8[6291456]{0:T(1024)(128)(4,1)} %bitcast.280), calls=%async_computation.6 | async-start | bytes 8388608
  150.7 2.2 collective-permute-start.20
  151.8 3.2 %collective-permute-start.22 = (bf16[64,2048]{1,0:T(8,128)(2,1)S(1)}, bf16[64,2048]{1,0:T(8,128)(2,1)S(1)}, u32[]{:S(2)}, u32[]{:S(2)}) collective-permute-start(bf16[64,2048]{1,0:T(8,128)(2,1)S(1)} %get-tuple-element.23), channel_id=1, source_target_pairs={{0,1},{1,0},{2,3},{3,2},{4,5},{5,4},{6,7},{7,6},{8,9},{9,8},{10,11... | collective-permute-start | bytes 786440 | tf_op jit(solution)/shard_map/ppermute | solution.py:47
  153.0 4.7 %collective-permute-start.21 = (bf16[32,2048]{1,0:T(8,128)(2,1)S(1)}, bf16[32,2048]{1,0:T(8,128)(2,1)S(1)}, u32[]{:S(2)}, u32[]{:S(2)}) collective-permute-start(bf16[32,2048]{1,0:T(8,128)(2,1)S(1)} %fusion.77), channel_id=1, source_target_pairs={{0,4},{4,8},{8,12},{12,14},{14,10},{10,6},{6,2},{2,0},{1,5},{5,9},... | collective-permute-start | bytes 393224 | tf_op jit(solution)/shard_map/ppermute | solution.py:56
  154.3 6.3 %collective-permute-start.24 = (bf16[64,2048]{1,0:T(8,128)(2,1)S(1)}, bf16[64,2048]{1,0:T(8,128)(2,1)S(1)}, u32[]{:S(2)}, u32[]{:S(2)}) collective-permute-start(bf16[64,2048]{1,0:T(8,128)(2,1)S(1)} %get-tuple-element.22), channel_id=1, source_target_pairs={{0,1},{1,0},{2,3},{3,2},{4,5},{5,4},{6,7},{7,6},{8,9},{9,8},{10,11... | collective-permute-start | bytes 786440 | tf_op jit(solution)/shard_map/ppermute | solution.py:47
  157.7 3.9 %collective-permute-start.23 = (bf16[32,2048]{1,0:T(8,128)(2,1)S(1)}, bf16[32,2048]{1,0:T(8,128)(2,1)S(1)}, u32[]{:S(2)}, u32[]{:S(2)}) collective-permute-start(bf16[32,2048]{1,0:T(8,128)(2,1)S(1)} %fusion.76), channel_id=1, source_target_pairs={{0,4},{4,8},{8,12},{12,14},{14,10},{10,6},{6,2},{2,0},{1,5},{5,9},... | collective-permute-start | bytes 393224 | tf_op jit(solution)/shard_map/ppermute | solution.py:56
  159.1 6.6 %collective-permute-start.26 = (bf16[64,2048]{1,0:T(8,128)(2,1)S(1)}, bf16[64,2048]{1,0:T(8,128)(2,1)S(1)}, u32[]{:S(2)}, u32[]{:S(2)}) collective-permute-start(bf16[64,2048]{1,0:T(8,128)(2,1)S(1)} %get-tuple-element.21), channel_id=1, source_target_pairs={{0,1},{1,0},{2,3},{3,2},{4,5},{5,4},{6,7},{7,6},{8,9},{9,8},{10,11... | collective-permute-start | bytes 786440 | tf_op jit(solution)/shard_map/ppermute | solution.py:47
  161.7 4.0 %collective-permute-start.25 = (bf16[32,2048]{1,0:T(8,128)(2,1)S(1)}, bf16[32,2048]{1,0:T(8,128)(2,1)S(1)}, u32[]{:S(2)}, u32[]{:S(2)}) collective-permute-start(bf16[32,2048]{1,0:T(8,128)(2,1)S(1)} %fusion.74), channel_id=1, source_target_pairs={{0,4},{4,8},{8,12},{12,14},{14,10},{10,6},{6,2},{2,0},{1,5},{5,9},... | collective-permute-start | bytes 393224 | tf_op jit(solution)/shard_map/ppermute | solution.py:56
  163.0 7.9 %collective-permute-start.28 = (bf16[64,2048]{1,0:T(8,128)(2,1)S(1)}, bf16[64,2048]{1,0:T(8,128)(2,1)S(1)}, u32[]{:S(2)}, u32[]{:S(2)}) collective-permute-start(bf16[64,2048]{1,0:T(8,128)(2,1)S(1)} %get-tuple-element.20), channel_id=1, source_target_pairs={{0,1},{1,0},{2,3},{3,2},{4,5},{5,4},{6,7},{7,6},{8,9},{9,8},{10,11... | collective-permute-start | bytes 786440 | tf_op jit(solution)/shard_map/ppermute | solution.py:47
  165.8 5.2 %collective-permute-start.27 = (bf16[32,2048]{1,0:T(8,128)(2,1)S(1)}, bf16[32,2048]{1,0:T(8,128)(2,1)S(1)}, u32[]{:S(2)}, u32[]{:S(2)}) collective-permute-start(bf16[32,2048]{1,0:T(8,128)(2,1)S(1)} %fusion.72), channel_id=1, source_target_pairs={{0,4},{4,8},{8,12},{12,14},{14,10},{10,6},{6,2},{2,0},{1,5},{5,9},... | collective-permute-start | bytes 393224 | tf_op jit(solution)/shard_map/ppermute | solution.py:56
  167.1 9.1 %collective-permute-start.30 = (bf16[64,2048]{1,0:T(8,128)(2,1)S(1)}, bf16[64,2048]{1,0:T(8,128)(2,1)S(1)}, u32[]{:S(2)}, u32[]{:S(2)}) collective-permute-start(bf16[64,2048]{1,0:T(8,128)(2,1)S(1)} %get-tuple-element.19), channel_id=1, source_target_pairs={{0,1},{1,0},{2,3},{3,2},{4,5},{5,4},{6,7},{7,6},{8,9},{9,8},{10,11... | collective-permute-start | bytes 786440 | tf_op jit(solution)/shard_map/ppermute | solution.py:47
  171.0 5.2 %collective-permute-start.29 = (bf16[32,2048]{1,0:T(8,128)(2,1)S(1)}, bf16[32,2048]{1,0:T(8,128)(2,1)S(1)}, u32[]{:S(2)}, u32[]{:S(2)}) collective-permute-start(bf16[32,2048]{1,0:T(8,128)(2,1)S(1)} %fusion.70), channel_id=1, source_target_pairs={{0,4},{4,8},{8,12},{12,14},{14,10},{10,6},{6,2},{2,0},{1,5},{5,9},... | collective-permute-start | bytes 393224 | tf_op jit(solution)/shard_map/ppermute | solution.py:56
  172.3 5.2 %collective-permute-start.32 = (bf16[64,2048]{1,0:T(8,128)(2,1)S(1)}, bf16[64,2048]{1,0:T(8,128)(2,1)S(1)}, u32[]{:S(2)}, u32[]{:S(2)}) collective-permute-start(bf16[64,2048]{1,0:T(8,128)(2,1)S(1)} %get-tuple-element.18), channel_id=1, source_target_pairs={{0,1},{1,0},{2,3},{3,2},{4,5},{5,4},{6,7},{7,6},{8,9},{9,8},{10,11... | collective-permute-start | bytes 786440 | tf_op jit(solution)/shard_map/ppermute | solution.py:47
  176.3 4.8 %collective-permute-start.31 = (bf16[32,2048]{1,0:T(8,128)(2,1)S(1)}, bf16[32,2048]{1,0:T(8,128)(2,1)S(1)}, u32[]{:S(2)}, u32[]{:S(2)}) collective-permute-start(bf16[32,2048]{1,0:T(8,128)(2,1)S(1)} %fusion.68), channel_id=1, source_target_pairs={{0,4},{4,8},{8,12},{12,14},{14,10},{10,6},{6,2},{2,0},{1,5},{5,9},... | collective-permute-start | bytes 393224 | tf_op jit(solution)/shard_map/ppermute | solution.py:56
  181.2 4.2 %collective-permute-start.35 = (bf16[32,2048]{1,0:T(8,128)(2,1)S(1)}, bf16[32,2048]{1,0:T(8,128)(2,1)S(1)}, u32[]{:S(2)}, u32[]{:S(2)}) collective-permute-start(bf16[32,2048]{1,0:T(8,128)(2,1)S(1)} %get-tuple-element.16), channel_id=1, source_target_pairs={{4,0},{8,4},{12,8},{14,12},{10,14},{6,10},{2,6},{0,2},{5,1},{9,5},... | collective-permute-start | bytes 393224 | tf_op jit(solution)/shard_map/ppermute | solution.py:57
  185.4 3.9 %collective-permute-start.36 = (bf16[32,2048]{1,0:T(8,128)(2,1)S(1)}, bf16[32,2048]{1,0:T(8,128)(2,1)S(1)}, u32[]{:S(2)}, u32[]{:S(2)}) collective-permute-start(bf16[32,2048]{1,0:T(8,128)(2,1)S(1)} %fusion.61), channel_id=1, source_target_pairs={{4,0},{8,4},{12,8},{14,12},{10,14},{6,10},{2,6},{0,2},{5,1},{9,5},... | collective-permute-start | bytes 393224 | tf_op jit(solution)/shard_map/ppermute | solution.py:57
  189.4 4.4 %collective-permute-start.37 = (bf16[32,2048]{1,0:T(8,128)(2,1)S(1)}, bf16[32,2048]{1,0:T(8,128)(2,1)S(1)}, u32[]{:S(2)}, u32[]{:S(2)}) collective-permute-start(bf16[32,2048]{1,0:T(8,128)(2,1)S(1)} %fusion.59), channel_id=1, source_target_pairs={{4,0},{8,4},{12,8},{14,12},{10,14},{6,10},{2,6},{0,2},{5,1},{9,5},... | collective-permute-start | bytes 393224 | tf_op jit(solution)/shard_map/ppermute | solution.py:57
  193.9 4.6 %collective-permute-start.38 = (bf16[32,2048]{1,0:T(8,128)(2,1)S(1)}, bf16[32,2048]{1,0:T(8,128)(2,1)S(1)}, u32[]{:S(2)}, u32[]{:S(2)}) collective-permute-start(bf16[32,2048]{1,0:T(8,128)(2,1)S(1)} %fusion.57), channel_id=1, source_target_pairs={{4,0},{8,4},{12,8},{14,12},{10,14},{6,10},{2,6},{0,2},{5,1},{9,5},... | collective-permute-start | bytes 393224 | tf_op jit(solution)/shard_map/ppermute | solution.py:57
  198.5 4.3 %collective-permute-start.39 = (bf16[32,2048]{1,0:T(8,128)(2,1)S(1)}, bf16[32,2048]{1,0:T(8,128)(2,1)S(1)}, u32[]{:S(2)}, u32[]{:S(2)}) collective-permute-start(bf16[32,2048]{1,0:T(8,128)(2,1)S(1)} %fusion.55), channel_id=1, source_target_pairs={{4,0},{8,4},{12,8},{14,12},{10,14},{6,10},{2,6},{0,2},{5,1},{9,5},... | collective-permute-start | bytes 393224 | tf_op jit(solution)/shard_map/ppermute | solution.py:57
  202.8 13.6 %collective-permute-start.40 = (bf16[32,2048]{1,0:T(8,128)(2,1)S(1)}, bf16[32,2048]{1,0:T(8,128)(2,1)S(1)}, u32[]{:S(2)}, u32[]{:S(2)}) collective-permute-start(bf16[32,2048]{1,0:T(8,128)(2,1)S(1)} %fusion.53), channel_id=1, source_target_pairs={{4,0},{8,4},{12,8},{14,12},{10,14},{6,10},{2,6},{0,2},{5,1},{9,5},... | collective-permute-start | bytes 393224 | tf_op jit(solution)/shard_map/ppermute | solution.py:57
  205.0 13.0 %collective-permute-start.34 = (bf16[64,2048]{1,0:T(8,128)(2,1)S(1)}, bf16[64,2048]{1,0:T(8,128)(2,1)S(1)}, u32[]{:S(2)}, u32[]{:S(2)}) collective-permute-start(bf16[64,2048]{1,0:T(8,128)(2,1)S(1)} %get-tuple-element.17), channel_id=1, source_target_pairs={{0,1},{1,0},{2,3},{3,2},{4,5},{5,4},{6,7},{7,6},{8,9},{9,8},{10,11... | collective-permute-start | bytes 786440 | tf_op jit(solution)/shard_map/ppermute | solution.py:47
  216.4 5.1 %collective-permute-start.33 = (bf16[32,2048]{1,0:T(8,128)(2,1)S(1)}, bf16[32,2048]{1,0:T(8,128)(2,1)S(1)}, u32[]{:S(2)}, u32[]{:S(2)}) collective-permute-start(bf16[32,2048]{1,0:T(8,128)(2,1)S(1)} %get-tuple-element.15), channel_id=1, source_target_pairs={{0,4},{4,8},{8,12},{12,14},{14,10},{10,6},{6,2},{2,0},{1,5},{5,9},... | collective-permute-start | bytes 393224 | tf_op jit(solution)/shard_map/ppermute | solution.py:56
  216.5 5.0 %collective-permute-start.41 = (bf16[32,2048]{1,0:T(8,128)(2,1)S(1)}, bf16[32,2048]{1,0:T(8,128)(2,1)S(1)}, u32[]{:S(2)}, u32[]{:S(2)}) collective-permute-start(bf16[32,2048]{1,0:T(8,128)(2,1)S(1)} %fusion.51), channel_id=1, source_target_pairs={{4,0},{8,4},{12,8},{14,12},{10,14},{6,10},{2,6},{0,2},{5,1},{9,5},... | collective-permute-start | bytes 393224 | tf_op jit(solution)/shard_map/ppermute | solution.py:57
  221.6 9.1 %collective-permute-start.42 = (bf16[64,2048]{1,0:T(8,128)(2,1)S(1)}, bf16[64,2048]{1,0:T(8,128)(2,1)S(1)}, u32[]{:S(2)}, u32[]{:S(2)}) collective-permute-start(bf16[64,2048]{1,0:T(8,128)(2,1)S(1)} %pad_maximum_fusion.3), channel_id=1, source_target_pairs={{0,0},{1,16},{16,17},{17,1},{2,2},{3,18},{18,19},{19,3},{4,4},{5,2... | collective-permute-start | bytes 786440 | tf_op jit(solution)/shard_map/ppermute | solution.py:63
  (6 other events, 12.1 us)
where the time goes:
time: 232 us; the launch traced here: 231 us
  waiting for transfers between devices  115 us (50%)
  starting transfers between devices  71.7 us (31%)
  matrix products  28.9 us (12%)
  local copies, waits for them, and re-layouts  9.42 us (4%)
  other arithmetic  6.2 us (3%)
    ppermute x2, waiting for transfers between devices, shards(): lax.ppermute(jnp.concatenate([g, u], axis=1).astype(jnp.bfloat16), 'dp',...  38.5 us
    ppermute x8, starting transfers between devices, ring_collect(): other[k] = lax.ppermute(away[k], 'etp', [(0, 1), (1, 0)])  25 us
    ppermute x4, waiting for transfers between devices, ring_spread(): up = lax.ppermute(up, 'expert', ahead)  22.8 us
    ppermute x2, waiting for transfers between devices, shards(): hidden[r].append(lax.ppermute(h, 'dp', perm))  18.5 us
    dot_general x8, matrix products, gate_up(): jnp.dot(packed[e], w[e], preferred_element_type=jnp.float32)  18.3 us
    ppermute x7, waiting for transfers between devices, ring_collect(): down = lax.ppermute(down, 'expert', back)  13.1 us
    ppermute x7, starting transfers between devices, ring_collect(): down = lax.ppermute(down, 'expert', back)  12 us
    ppermute x7, waiting for transfers between devices, ring_collect(): up = lax.ppermute(up, 'expert', ahead)  10.8 us
  transfers between devices with their start and end apart: 43, of which 21 were waited for; matrix products, arithmetic and copies ran while one was open for 8% of the time, Pallas kernels for 0%

commit v1 on v0

--- a/solution.py
+++ b/solution.py
@@ -1,66 +1,309 @@
+import functools
+
 import jax
 import jax.numpy as jnp
 from jax import lax
+from jax.experimental import pallas as pl
+from jax.experimental.pallas import tpu as pltpu
 from jax.sharding import PartitionSpec as P
 
-
-def ring_steps(columns):
-    ring = list(range(0, columns, 2)) + list(range(1, columns, 2))[::-1]
-    ahead = [(ring[i], ring[(i + 1) % columns]) for i in range(columns)]
-    return ahead, [(b, a) for a, b in ahead]
-
-
-def ring_spread(block, groups, columns, cores):
-    perm = [
-        (((d - c) % groups) * cores + d, d * cores + c) for d in range(groups) for c in range(cores)
-    ]
-    ahead, back = ring_steps(columns)
-    block = lax.ppermute(block, ("dp", "etp"), perm)
-    held = {0: block}
-    up = down = block
-    for step in range(1, columns // 2 + 1):
-        up = lax.ppermute(up, "expert", ahead)
-        held[step] = up
-        if columns - step > step:
-            down = lax.ppermute(down, "expert", back)
-            held[columns - step] = down
-    swap = [(0, 1), (1, 0)]
-    other = {k: lax.ppermute(held[k], "etp", swap) for k in held}
-    first = lax.axis_index("etp") == 0
-    pairs = [(held[k], other[k]) for k in range(columns)]
-    return (
-        jnp.stack([jnp.where(first, a, b) for a, b in pairs]),
-        jnp.stack([jnp.where(first, b, a) for a, b in pairs]),
-    )
-
-
-def ring_collect(parts, groups, columns, cores):
-    ahead, back = ring_steps(columns)
-    first = lax.axis_index("etp") == 0
-    mine = jnp.where(first, parts[0], parts[1])
-    away = jnp.where(first, parts[1], parts[0])
-    half = mine.shape[1] // 2
-    order = [k for s in range(1, columns // 2 + 1) for k in (s, columns - s)] + [0]
-    other = {}
-    for k in order:
-        if k not in other:
-            other[k] = lax.ppermute(away[k], "etp", [(0, 1), (1, 0)])
-
-    def own(k, low):
-        rows = slice(0, half) if low else slice(half, None)
-        return mine[k, rows].astype(jnp.float32) + other[k][rows].astype(jnp.float32)
-
-    up = own(1, True).astype(jnp.bfloat16)
-    down = own(columns - 1, False).astype(jnp.bfloat16)
-    for step in range(2, columns + 1):
-        up = lax.ppermute(up, "expert", ahead)
-        down = lax.ppermute(down, "expert", back)
-        up = (up.astype(jnp.float32) + own(step % columns, True)).astype(jnp.bfloat16)
-        down = (down.astype(jnp.float32) + own(columns - step, False)).astype(jnp.bfloat16)
-    perm = [
-        (d * cores + c, ((d - c) % groups) * cores + d) for d in range(groups) for c in range(cores)
-    ]
-    return lax.ppermute(jnp.concatenate([up, down]), ("dp", "etp"), perm)
+MESH = pl.DeviceIdType.MESH
+RING, RING_META, SIDE, SIDE_META, PART, HIDDEN, OUT, SUM = 0, 1, 2, 3, 4, 6, 7, 8
+KINDS = 9
+
+
+def chunks(size, most):
+    step = most if size % most == 0 else 128
+    return [slice(n, n + step) for n in range(0, size, step)]
+
+
+def layer_kernel(
+    columns, experts, capacity,
+    tokens, meta, gate, up, down, result,
+    tok, met, wg, wu, wd, xs, pick, own, psend, precv, hid, dense,
+    keep, osend, orecv, ssend, srecv, final, sent, got, local,
+):
+    d, i, c = lax.axis_index("dp"), lax.axis_index("expert"), lax.axis_index("etp")
+    held, width, share = wg.shape
+    rows = tok.shape[2]
+    half, last = columns // 2, columns - 1
+    odd, line = i % 2, i // 2
+    place = (1 - odd) * line + odd * (last - line)
+
+    def at(p):
+        p = (p + columns) % columns
+        b = p // half
+        return (1 - b) * (2 * p) + b * (2 * (last - p) + 1)
+
+    way = 1 - 2 * c
+    ahead, behind = (d, at(place + way), c), (d, at(place - way), c)
+    side, across, corner = (d, i, 1 - c), (1 - d, i, c), (1 - d, i, 1 - c)
+
+    def remote(src, dst, kind, s, r, device):
+        return pltpu.make_async_remote_copy(
+            src_ref=src, dst_ref=dst, send_sem=sent.at[kind, s], recv_sem=got.at[kind, r],
+            device_id=device, device_id_type=MESH,
+        )
+
+    def ring_tok(s):
+        return remote(tok.at[s, c], tok.at[s + 1, c], RING, s, s + 1, ahead)
+
+    def ring_meta(s):
+        return remote(met.at[s, c], met.at[s + 1, c], RING_META, s, s + 1, ahead)
+
+    def side_tok(s, g):
+        return remote(tok.at[s, g], tok.at[s, g], SIDE, s, s, side)
+
+    def side_meta(s, g):
+        return remote(met.at[s, g], met.at[s, g], SIDE_META, s, s, side)
+
+    def part_copy(s, e):
+        return remote(psend.at[s, e], precv.at[s, e], PART + e, s, s, across)
+
+    def hidden_copy(s):
+        return remote(hid.at[s, 0], hid.at[s, 1], HIDDEN, s, s, across)
+
+    def out_copy(s):
+        return remote(osend.at[s], orecv.at[s], OUT, s, s, side)
+
+    def sum_copy(s, after):
+        return remote(ssend.at[s], srecv.at[after], SUM, s, after, ahead)
+
+    weights = []
+    for e in range(held):
+        weights.append(pltpu.make_async_copy(gate.at[e], wg.at[e], local.at[len(weights)]))
+        weights.append(pltpu.make_async_copy(up.at[e], wu.at[e], local.at[len(weights)]))
+    weights.append(pltpu.make_async_copy(down, wd, local.at[len(weights)]))
+    first_tok = pltpu.make_async_copy(tokens, tok.at[0, c], local.at[len(weights)])
+    first_meta = pltpu.make_async_copy(meta, met.at[0, c], local.at[len(weights) + 1])
+    move_tok = remote(tokens, tok.at[0, d], RING, last, 0, corner)
+    move_meta = remote(meta, met.at[0, d], RING_META, last, 0, corner)
+    got_tok = remote(tokens, tok.at[0, c], RING, last, 0, corner)
+    got_meta = remote(meta, met.at[0, c], RING_META, last, 0, corner)
+
+    @pl.when(c == d)
+    def _():
+        first_tok.start()
+        first_meta.start()
+
+    for w in weights:
+        w.start()
+    barrier = pltpu.get_barrier_semaphore()
+    for device in (ahead, behind, side, across, corner):
+        pl.semaphore_signal(barrier, inc=1, device_id=device, device_id_type=MESH)
+    pl.semaphore_wait(barrier, 5)
+
+    @pl.when(c != d)
+    def _():
+        move_tok.start()
+        move_meta.start()
+        got_tok.wait_recv()
+        got_meta.wait_recv()
+
+    @pl.when(c == d)
+    def _():
+        first_tok.wait()
+        first_meta.wait()
+
+    lane = lax.broadcasted_iota(jnp.int32, (1, 2 * rows), 1)
+    in_first = lane < rows
+    mine = (lane >= d * rows) & (lane < (d + 1) * rows)
+    slots = lax.broadcasted_iota(jnp.int32, (capacity, 2 * rows), 0).astype(jnp.float32)
+
+    def row_of(s, r):
+        return jnp.where(in_first, met[s, 0, pl.ds(r, 1), :], met[s, 1, pl.ds(r, 1), :])
+
+    def front(s):
+        @pl.when(s > 0)
+        def _():
+            ring_tok(s - 1).wait_recv()
+            ring_meta(s - 1).wait_recv()
+
+        @pl.when(s < last)
+        def _():
+            ring_tok(s).start()
+            ring_meta(s).start()
+
+        side_tok(s, c).start()
+        side_meta(s, c).start()
+        side_tok(s, 1 - c).wait_recv()
+        side_meta(s, 1 - c).wait_recv()
+        for e in range(held):
+            hit = slots == row_of(s, held * i + e)
+            pick[s, e, :capacity] = (hit & mine).astype(jnp.bfloat16)
+            pick[s, e, capacity:] = (hit & ~mine).astype(jnp.bfloat16)
+        picker = pick[s].reshape(held * 2 * capacity, 2 * rows)
+        for n in chunks(width, 256):
+            packed = jnp.dot(
+                picker, tok[s, :, :, n].reshape(2 * rows, -1), preferred_element_type=jnp.float32
+            )
+            xs[:, :, n] = packed.astype(jnp.bfloat16).reshape(held, 2 * capacity, -1)
+        for e in range(held):
+            @pl.when(s == 0)
+            def _():
+                weights[2 * e].wait()
+                weights[2 * e + 1].wait()
+
+            for k, w in enumerate((wg, wu)):
+                for n in chunks(share, 256):
+                    v = jnp.dot(xs[e], w[e, :, n], preferred_element_type=jnp.float32)
+                    to = slice(k * share + n.start, k * share + n.stop)
+                    own[s, e, :, to] = v[:capacity]
+                    psend[s, e, :, to] = v[capacity:].astype(jnp.bfloat16)
+            part_copy(s, e).start()
+
+    def middle(s):
+        for e in range(held):
+            part_copy(s, e).wait_recv()
+            hit = (slots == row_of(s, held * i + e)) & mine
+            scale = row_of(s, experts + held * i + e)
+            scale = jnp.sum(jnp.where(hit, scale, 0.0), axis=1, keepdims=True)
+            for n in chunks(share, 256):
+                to = slice(share + n.start, share + n.stop)
+                g = own[s, e, :, n] + precv[s, e, :, n].astype(jnp.float32)
+                u = own[s, e, :, to] + precv[s, e, :, to].astype(jnp.float32)
+                h = g / (1.0 + jnp.exp(-g)) * u * scale
+                hid[s, 0, e, :, n] = h.astype(jnp.bfloat16)
+        hidden_copy(s).start()
+
+    def back(s):
+        @pl.when(s == 0)
+        def _():
+            weights[-1].wait()
+
+        hidden_copy(s).wait_recv()
+        for e in range(held):
+            for n in chunks(share, 256):
+                h = jnp.concatenate([hid[s, 0, e, :, n], hid[s, 1, e, :, n]], axis=0)
+                spread = lax.dot_general(
+                    pick[s, e], h, (((0,), (0,)), ((), ())), preferred_element_type=jnp.float32
+                )
+                dense[:, e * share + n.start : e * share + n.stop] = spread.astype(jnp.bfloat16)
+        for n in chunks(width, 256):
+            v = jnp.dot(
+                dense[...], wd[:, :, n].reshape(held * share, -1),
+                preferred_element_type=jnp.float32,
+            )
+            low, high = v[:rows], v[rows:]
+            keep[s, :, n] = jnp.where(c == 0, low, high)
+            osend[s, :, n] = jnp.where(c == 0, high, low).astype(jnp.bfloat16)
+        out_copy(s).start()
+
+    def total(s, n):
+        return keep[s, :, n] + orecv[s, :, n].astype(jnp.float32)
+
+    def collect(s):
+        out_copy(s).wait_recv()
+
+        @pl.when(s == 1)
+        def _():
+            for n in chunks(width, 512):
+                ssend[s, :, n] = total(s, n).astype(jnp.bfloat16)
+
+        @pl.when(s > 1)
+        def _():
+            sum_copy(s - 1, s).wait_recv()
+            for n in chunks(width, 512):
+                v = total(s, n) + srecv[s, :, n].astype(jnp.float32)
+                ssend[s, :, n] = v.astype(jnp.bfloat16)
+
+        sum_copy(s, (s + 1) % columns).start()
+
+    def turn(t, carry):
+        pl.when(t < columns)(lambda: front(t))
+        pl.when((t >= 1) & (t < columns + 1))(lambda: middle(t - 1))
+        pl.when((t >= 2) & (t < columns + 2))(lambda: back(t - 2))
+        pl.when(t >= 4)(lambda: collect(t - 3))
+        return carry
+
+    lax.fori_loop(0, columns + 3, turn, 0)
+
+    out_copy(0).wait_recv()
+    sum_copy(last, 0).wait_recv()
+    for n in chunks(width, 512):
+        v = total(0, n) + srecv[0, :, n].astype(jnp.float32)
+        final[:, n] = v.astype(jnp.bfloat16)
+    give = remote(final, result, SUM, 0, 1, corner)
+    stay = pltpu.make_async_copy(final, result, local.at[0])
+
+    @pl.when(c == d)
+    def _():
+        stay.start()
+        stay.wait()
+
+    @pl.when(c != d)
+    def _():
+        give.start()
+        move_tok.wait_send()
+        move_meta.wait_send()
+        give.wait()
+
+    def settle(s, carry):
+        @pl.when(s < last)
+        def _():
+            ring_tok(s).wait_send()
+            ring_meta(s).wait_send()
+
+        side_tok(s, c).wait_send()
+        side_meta(s, c).wait_send()
+        for e in range(held):
+            part_copy(s, e).wait_send()
+        hidden_copy(s).wait_send()
+        out_copy(s).wait_send()
+
+        @pl.when(s > 0)
+        def _():
+            sum_copy(s, (s + 1) % columns).wait_send()
+
+        return carry
+
+    lax.fori_loop(0, columns, settle, 0)
+
+
+def near_layer(tokens, expert_ids, combine, gate, up, down, columns, experts, capacity):
+    rows, width = tokens.shape
+    held, depth, share = gate.shape
+    named = expert_ids[:, :, None] == jnp.arange(experts, dtype=jnp.int32)[None, None, :]
+    weight = jnp.sum(jnp.where(named, combine[:, :, None], 0.0), axis=1).T
+    chosen = jnp.any(named, axis=1).T
+    earlier = jnp.triu(jnp.ones((rows, rows), jnp.bfloat16), 1)
+    slot = jnp.dot(chosen.astype(jnp.bfloat16), earlier, preferred_element_type=jnp.float32)
+    slot = jnp.where(chosen, slot, -1.0)
+    meta = jnp.concatenate([slot, weight])
+    meta = jnp.concatenate([meta, meta], axis=1)
+    bf16, f32 = jnp.bfloat16, jnp.float32
+    return pl.pallas_call(
+        functools.partial(layer_kernel, columns, experts, capacity),
+        out_shape=jax.ShapeDtypeStruct((rows, width), bf16),
+        in_specs=[pl.BlockSpec(memory_space=pl.ANY)] * 5,
+        out_specs=pl.BlockSpec(memory_space=pl.ANY),
+        scratch_shapes=[
+            pltpu.VMEM((columns, 2, rows, width), bf16),
+            pltpu.VMEM((columns, 2, 2 * experts, 2 * rows), f32),
+            pltpu.VMEM(gate.shape, bf16),
+            pltpu.VMEM(up.shape, bf16),
+            pltpu.VMEM(down.shape, bf16),
+            pltpu.VMEM((held, 2 * capacity, width), bf16),
+            pltpu.VMEM((columns, held, 2 * capacity, 2 * rows), bf16),
+            pltpu.VMEM((columns, held, capacity, 2 * share), f32),
+            pltpu.VMEM((columns, held, capacity, 2 * share), bf16),
+            pltpu.VMEM((columns, held, capacity, 2 * share), bf16),
+            pltpu.VMEM((columns, 2, held, capacity, share), bf16),
+            pltpu.VMEM((2 * rows, held * share), bf16),
+            pltpu.VMEM((columns, rows, width), f32),
+            pltpu.VMEM((columns, rows, width), bf16),
+            pltpu.VMEM((columns, rows, width), bf16),
+            pltpu.VMEM((columns, rows, width), bf16),
+            pltpu.VMEM((columns, rows, width), bf16),
+            pltpu.VMEM((rows, width), bf16),
+            pltpu.SemaphoreType.DMA((KINDS, columns)),
+            pltpu.SemaphoreType.DMA((KINDS, columns)),
+            pltpu.SemaphoreType.DMA((2 * held + 3,)),
+        ],
+        compiler_params=pltpu.CompilerParams(
+            collective_id=0, has_side_effects=True, vmem_limit_bytes=67043328
+        ),
+    )(tokens, meta, gate, up, down)
 
 
 def spread_tokens(tokens, groups, cores, width):
@@ -116,24 +359,15 @@
     capacity = min(rows, 3 * rows * top_count // (2 * experts))
     group = lax.axis_index("dp")
 
+    if groups == cores == 2 and columns % 2 == 0 and capacity % 16 == 0:
+        return near_layer(
+            tokens, expert_ids, combine, gate_weight, up_weight, down_weight,
+            columns, experts, capacity,
+        )
     named = expert_ids[:, :, None] == jnp.arange(experts, dtype=jnp.int32)[None, None, :]
     weight = jnp.sum(jnp.where(named, combine[:, :, None], 0.0), axis=1)
-    near = groups == cores == 2 and columns % 2 == 0
-    if near:
-        high = weight.T.astype(jnp.bfloat16)
-        low = (weight.T - high.astype(jnp.float32)).astype(jnp.bfloat16)
-        extra = jnp.stack([high, low]).reshape(-1)
-        extra_rows = -(-extra.size // (8 * tokens.shape[1])) * 8
-        extra = jnp.pad(extra, (0, extra_rows * tokens.shape[1] - extra.size))
-        block = jnp.concatenate([tokens, extra.reshape(extra_rows, -1)])
-        whole = ring_spread(block, groups, columns, cores)
-        spread = [a[:, :rows] for a in whole]
-        tail = jnp.stack([a[:, rows:] for a in whole]).reshape(groups * columns, -1)
-        tail = tail[:, : 2 * experts * rows].reshape(-1, 2, experts, rows).astype(jnp.float32)
-        weight = tail[:, 0] + tail[:, 1]
-    else:
-        spread = spread_tokens(tokens, groups, cores, width)
-        weight = lax.all_gather(weight.T, ("dp", "expert"), axis=0)
+    spread = spread_tokens(tokens, groups, cores, width)
+    weight = lax.all_gather(weight.T, ("dp", "expert"), axis=0)
     weight = lax.dynamic_slice_in_dim(weight, lax.axis_index("expert") * held, held, axis=1)
     chosen = (weight > 0).astype(jnp.bfloat16)
     earlier = jnp.triu(jnp.ones((rows, rows), jnp.bfloat16), 1)
@@ -145,7 +379,7 @@
     slot_weight = slot_weight.reshape(groups, columns, held, capacity)
 
     def pick(r):
-        which = r if near else jnp.mod(group - r, groups)
+        which = jnp.mod(group - r, groups)
         return lax.dynamic_index_in_dim(picker, which, 0, keepdims=False)
 
     def gate_up(r):
@@ -174,7 +408,7 @@
             half = sent.shape[1] // 2
             gates[e].append(sent[:, :half].astype(jnp.float32))
             ups[e].append(sent[:, half:].astype(jnp.float32))
-    own_weight = lax.dynamic_index_in_dim(slot_weight, 0 if near else group, 0, keepdims=False)
+    own_weight = lax.dynamic_index_in_dim(slot_weight, group, 0, keepdims=False)
     own_weight = own_weight.transpose(1, 0, 2).reshape(held, columns * capacity, 1)
     hidden = [[] for _ in range(groups)]
     for e, (g, u) in enumerate(gate_up(0)):
@@ -195,8 +429,6 @@
             dense, down_weight.reshape(-1, width), preferred_element_type=jnp.float32
         )
         parts.append(out.astype(jnp.bfloat16).reshape(columns, rows, width))
-    if near:
-        return ring_collect(parts, groups, columns, cores)
     return collect_output(parts, groups, cores, width)
 
 

time: 232 us -> 116 us (0.50)
  waiting for transfers between devices: 115 us -> 0 us
  Pallas kernels: 0 us -> 112 us
  starting transfers between devices: 71.7 us -> 0 us
  matrix products: 28.9 us -> 0.13 us
  local copies, waits for them, and re-layouts: 9.42 us -> 1.67 us
  other arithmetic: 6.2 us -> 2.11 us
    ppermute x43 -> x0, waiting for transfers between devices: 115 us -> none  [the longest x2 38.5 us: shards(): lax.ppermute(jnp.concatenate([g, u], axis=1).astype(jnp.bfloat16), 'dp',...]
    pallas_call x0 -> x1, Pallas kernels: none -> 112 us  [near_layer(): pl.pallas_call(functools.partial(layer_kernel, columns, experts, capacity...]
    ppermute x43 -> x0, starting transfers between devices: 71.7 us -> none  [the longest x8 25 us: ring_collect(): other[k] = lax.ppermute(away[k], 'etp', [(0, 1), (1, 0)])]
    dot_general x15 -> x1, matrix products: 28.9 us -> 0.13 us  [near_layer(): jnp.dot(chosen.astype(jnp.bfloat16), earlier, preferred_element_type=jnp....]
    convert_element_type x3 -> x0, local copies, waits for them, and re-layouts: 3.34 us -> none  [the longest x2 3.24 us: shards(): dense = dense.astype(jnp.bfloat16).reshape(columns * rows, -1)]
    unnamed x26 -> x1, local copies, waits for them, and re-layouts: 4.81 us -> 1.67 us
    concatenate x4 -> x1, other arithmetic: 3.29 us -> 0.68 us  [near_layer(): meta = jnp.concatenate([meta, meta], axis=1)]
  transfers between devices with their start and end apart: 43 -> 0, of which waited for: 21 -> 0; matrix products, arithmetic and copies ran while one was open for 8% -> 0% of each run, Pallas kernels for 0% -> 0%
where the time goes in v1:
time: 116 us; the launch traced here: 115 us
  Pallas kernels  112 us (97%)
  other arithmetic  2.11 us (2%)
  local copies, waits for them, and re-layouts  1.67 us (1%)
    pallas_call x1, Pallas kernels, near_layer(): pl.pallas_call(functools.partial(layer_kernel, columns, experts, capacity...  112 us

profile of v1, /device:TPU:1, one launch (start us, length us, event | category | flops | bytes accessed | tf_op | source)
XLA Modules:
  0.0 115.4 jit_solution(4261226905176921798)
XLA Ops:
  0.0 0.7 fusion
  0.7 0.1 convolution_select_fusion
  0.8 0.7 select_reduce_fusion
  1.6 0.7 maximum_maximum_fusion.meta
  2.2 111.5 %shard_map.64 = bf16[64,2048]{1,0:T(8,128)(2,1)} custom-call(bf16[64,2048]{1,0:T(8,128)(2,1)} %tokens.1, f32[32,128]{1,0:T(8,128)} %maximum_maximum_fusion.meta, bf16[2,2048,768]{2,1,0:T(8,128)(2,1)} %gate.1, bf16[2,2048,768]{2,1,0:T(8,128)(2,1)} %up.1, bf16[2,768,2048]{2,1,0:T(8,128)(2,1)} %down.1), custom_call_target="tpu_custom_call" | custom-call | tf_op jit(solution)/shard_map/pallas_call | solution.py:275
  113.8 1.7 %copy.10 = bf16[64,2048]{1,0:T(8,128)(2,1)} copy(bf16[64,2048]{1,0:T(8,128)(2,1)} %shard_map.64) | data formatting | bytes 524288

commit v2 on v1

--- a/solution.py
+++ b/solution.py
@@ -8,8 +8,8 @@
 from jax.sharding import PartitionSpec as P
 
 MESH = pl.DeviceIdType.MESH
-RING, RING_META, SIDE, SIDE_META, PART, HIDDEN, OUT, SUM = 0, 1, 2, 3, 4, 6, 7, 8
-KINDS = 9
+RING, RING_META, SIDE, SIDE_META, HIDDEN = 0, 1, 2, 3, 4
+PIECES = 4
 
 
 def chunks(size, most):
@@ -17,15 +17,34 @@
     return [slice(n, n + step) for n in range(0, size, step)]
 
 
+def routing_rows(ids, combine, experts):
+    rows, top = ids.shape
+    lane = lax.broadcasted_iota(jnp.int32, (rows, 128), 1)
+    weight = jnp.zeros((rows, 128), jnp.float32)
+    chosen = jnp.zeros((rows, 128), jnp.float32)
+    for k in range(top):
+        same = lane == ids[:, k : k + 1]
+        weight = jnp.where(same, combine[:, k : k + 1], weight)
+        chosen = jnp.where(same, 1.0, chosen)
+    before = lax.broadcasted_iota(jnp.int32, (rows, rows), 1)
+    before = (before < lax.broadcasted_iota(jnp.int32, (rows, rows), 0)).astype(jnp.bfloat16)
+    slot = jnp.dot(before, chosen.astype(jnp.bfloat16), preferred_element_type=jnp.float32)
+    slot = jnp.where(chosen > 0, slot, -1.0)
+    return [jnp.concatenate([a, a]).T[:experts] for a in (slot, weight)]
+
+
 def layer_kernel(
     columns, experts, capacity,
-    tokens, meta, gate, up, down, result,
-    tok, met, wg, wu, wd, xs, pick, own, psend, precv, hid, dense,
-    keep, osend, orecv, ssend, srecv, final, sent, got, local,
+    tokens, ids, combine, gate, up, down, result,
+    tok, met, stage, mstage, idv, cov, wg, wu, wd, xs, pick, own, psend, precv, hid, dense,
+    keep, osend, orecv, ssend, srecv, final, sent, got, psent, pgot, osent, ogot, ssent, sgot,
+    fsent, fgot, local,
 ):
     d, i, c = lax.axis_index("dp"), lax.axis_index("expert"), lax.axis_index("etp")
     held, width, share = wg.shape
     rows = tok.shape[2]
+    parts, piece = own.shape[2], own.shape[4] // 2
+    span = width // PIECES
     half, last = columns // 2, columns - 1
     odd, line = i % 2, i // 2
     place = (1 - odd) * line + odd * (last - line)
@@ -39,12 +58,15 @@
     ahead, behind = (d, at(place + way), c), (d, at(place - way), c)
     side, across, corner = (d, i, 1 - c), (1 - d, i, c), (1 - d, i, 1 - c)
 
-    def remote(src, dst, kind, s, r, device):
+    def copy(src, dst, send, recv, device):
         return pltpu.make_async_remote_copy(
-            src_ref=src, dst_ref=dst, send_sem=sent.at[kind, s], recv_sem=got.at[kind, r],
+            src_ref=src, dst_ref=dst, send_sem=send, recv_sem=recv,
             device_id=device, device_id_type=MESH,
         )
 
+    def remote(src, dst, kind, s, r, device):
+        return copy(src, dst, sent.at[kind, s], got.at[kind, r], device)
+
     def ring_tok(s):
         return remote(tok.at[s, c], tok.at[s + 1, c], RING, s, s + 1, ahead)
 
@@ -57,40 +79,63 @@
     def side_meta(s, g):
         return remote(met.at[s, g], met.at[s, g], SIDE_META, s, s, side)
 
-    def part_copy(s, e):
-        return remote(psend.at[s, e], precv.at[s, e], PART + e, s, s, across)
+    def part_copy(s, e, p):
+        k = e * parts + p
+        return copy(psend.at[s, e, p], precv.at[s, e, p], psent.at[k, s], pgot.at[k, s], across)
 
     def hidden_copy(s):
         return remote(hid.at[s, 0], hid.at[s, 1], HIDDEN, s, s, across)
 
-    def out_copy(s):
-        return remote(osend.at[s], orecv.at[s], OUT, s, s, side)
-
-    def sum_copy(s, after):
-        return remote(ssend.at[s], srecv.at[after], SUM, s, after, ahead)
+    def out_copy(s, q):
+        return copy(osend.at[s, q], orecv.at[s, q], osent.at[q, s], ogot.at[q, s], side)
+
+    def sum_copy(s, after, q):
+        return copy(ssend.at[s, q], srecv.at[after, q], ssent.at[q, s], sgot.at[q, after], ahead)
+
+    def give_copy(q):
+        cols = pl.ds(q * span, span)
+        return copy(final.at[:, cols], result.at[:, cols], fsent.at[q], fgot.at[q], corner)
 
     weights = []
     for e in range(held):
         weights.append(pltpu.make_async_copy(gate.at[e], wg.at[e], local.at[len(weights)]))
         weights.append(pltpu.make_async_copy(up.at[e], wu.at[e], local.at[len(weights)]))
     weights.append(pltpu.make_async_copy(down, wd, local.at[len(weights)]))
-    first_tok = pltpu.make_async_copy(tokens, tok.at[0, c], local.at[len(weights)])
-    first_meta = pltpu.make_async_copy(meta, met.at[0, c], local.at[len(weights) + 1])
-    move_tok = remote(tokens, tok.at[0, d], RING, last, 0, corner)
-    move_meta = remote(meta, met.at[0, d], RING_META, last, 0, corner)
-    got_tok = remote(tokens, tok.at[0, c], RING, last, 0, corner)
-    got_meta = remote(meta, met.at[0, c], RING_META, last, 0, corner)
-
-    @pl.when(c == d)
-    def _():
-        first_tok.start()
-        first_meta.start()
-
-    for w in weights:
-        w.start()
+    free = len(weights)
+    ids_copy = pltpu.make_async_copy(ids, idv, local.at[free])
+    combine_copy = pltpu.make_async_copy(combine, cov, local.at[free + 1])
+    keep_tok = pltpu.make_async_copy(tokens, tok.at[0, c], local.at[free + 2])
+    stage_tok = pltpu.make_async_copy(tokens, stage, local.at[free + 2])
+    move_tok = remote(stage, tok.at[0, d], RING, last, 0, corner)
+    move_meta = remote(mstage, met.at[0, d], RING_META, last, 0, corner)
+    got_tok = remote(stage, tok.at[0, c], RING, last, 0, corner)
+    got_meta = remote(mstage, met.at[0, c], RING_META, last, 0, corner)
+
     barrier = pltpu.get_barrier_semaphore()
     for device in (ahead, behind, side, across, corner):
         pl.semaphore_signal(barrier, inc=1, device_id=device, device_id_type=MESH)
+    ids_copy.start()
+    combine_copy.start()
+    pl.when(c == d)(lambda: keep_tok.start())
+    pl.when(c != d)(lambda: stage_tok.start())
+    for w in weights:
+        w.start()
+    ids_copy.wait()
+    combine_copy.wait()
+    slot_rows, weight_rows = routing_rows(idv[...], cov[...], experts)
+
+    @pl.when(c == d)
+    def _():
+        met[0, c, :experts] = slot_rows
+        met[0, c, experts:] = weight_rows
+        keep_tok.wait()
+
+    @pl.when(c != d)
+    def _():
+        mstage[:experts] = slot_rows
+        mstage[experts:] = weight_rows
+        stage_tok.wait()
+
     pl.semaphore_wait(barrier, 5)
 
     @pl.when(c != d)
@@ -100,11 +145,6 @@
         got_tok.wait_recv()
         got_meta.wait_recv()
 
-    @pl.when(c == d)
-    def _():
-        first_tok.wait()
-        first_meta.wait()
-
     lane = lax.broadcasted_iota(jnp.int32, (1, 2 * rows), 1)
     in_first = lane < rows
     mine = (lane >= d * rows) & (lane < (d + 1) * rows)
@@ -119,13 +159,14 @@
             ring_tok(s - 1).wait_recv()
             ring_meta(s - 1).wait_recv()
 
+        side_tok(s, c).start()
+        side_meta(s, c).start()
+
         @pl.when(s < last)
         def _():
             ring_tok(s).start()
             ring_meta(s).start()
 
-        side_tok(s, c).start()
-        side_meta(s, c).start()
         side_tok(s, 1 - c).wait_recv()
         side_meta(s, 1 - c).wait_recv()
         for e in range(held):
@@ -144,33 +185,33 @@
                 weights[2 * e].wait()
                 weights[2 * e + 1].wait()
 
-            for k, w in enumerate((wg, wu)):
-                for n in chunks(share, 256):
-                    v = jnp.dot(xs[e], w[e, :, n], preferred_element_type=jnp.float32)
-                    to = slice(k * share + n.start, k * share + n.stop)
-                    own[s, e, :, to] = v[:capacity]
-                    psend[s, e, :, to] = v[capacity:].astype(jnp.bfloat16)
-            part_copy(s, e).start()
+            for p in range(parts):
+                for k, w in enumerate((wg, wu)):
+                    v = jnp.dot(
+                        xs[e], w[e, :, p * piece : (p + 1) * piece],
+                        preferred_element_type=jnp.float32,
+                    )
+                    to = slice(k * piece, (k + 1) * piece)
+                    own[s, e, p, :, to] = v[:capacity]
+                    psend[s, e, p, :, to] = v[capacity:].astype(jnp.bfloat16)
+                part_copy(s, e, p).start()
 
     def middle(s):
         for e in range(held):
-            part_copy(s, e).wait_recv()
             hit = (slots == row_of(s, held * i + e)) & mine
             scale = row_of(s, experts + held * i + e)
             scale = jnp.sum(jnp.where(hit, scale, 0.0), axis=1, keepdims=True)
-            for n in chunks(share, 256):
-                to = slice(share + n.start, share + n.stop)
-                g = own[s, e, :, n] + precv[s, e, :, n].astype(jnp.float32)
-                u = own[s, e, :, to] + precv[s, e, :, to].astype(jnp.float32)
+            for p in range(parts):
+                part_copy(s, e, p).wait_recv()
+                g = own[s, e, p, :, :piece] + precv[s, e, p, :, :piece].astype(jnp.float32)
+                u = own[s, e, p, :, piece:] + precv[s, e, p, :, piece:].astype(jnp.float32)
                 h = g / (1.0 + jnp.exp(-g)) * u * scale
-                hid[s, 0, e, :, n] = h.astype(jnp.bfloat16)
-        hidden_copy(s).start()
+                hid[s, 0, e, :, p * piece : (p + 1) * piece] = h.astype(jnp.bfloat16)
+
+        pl.when(s > 0)(lambda: hidden_copy(s).start())
+        pl.when(s == last)(lambda: hidden_copy(0).start())
 
     def back(s):
-        @pl.when(s == 0)
-        def _():
-            weights[-1].wait()
-
         hidden_copy(s).wait_recv()
         for e in range(held):
             for n in chunks(share, 256):
@@ -179,52 +220,59 @@
                     pick[s, e], h, (((0,), (0,)), ((), ())), preferred_element_type=jnp.float32
                 )
                 dense[:, e * share + n.start : e * share + n.stop] = spread.astype(jnp.bfloat16)
-        for n in chunks(width, 256):
-            v = jnp.dot(
-                dense[...], wd[:, :, n].reshape(held * share, -1),
-                preferred_element_type=jnp.float32,
-            )
-            low, high = v[:rows], v[rows:]
-            keep[s, :, n] = jnp.where(c == 0, low, high)
-            osend[s, :, n] = jnp.where(c == 0, high, low).astype(jnp.bfloat16)
-        out_copy(s).start()
-
-    def total(s, n):
-        return keep[s, :, n] + orecv[s, :, n].astype(jnp.float32)
+        for q in range(PIECES):
+            for n in chunks(span, 256):
+                v = jnp.dot(
+                    dense[...],
+                    wd[:, :, q * span + n.start : q * span + n.stop].reshape(held * share, -1),
+                    preferred_element_type=jnp.float32,
+                )
+                low, high = v[:rows], v[rows:]
+                keep[s, q, :, n] = jnp.where(c == 0, low, high)
+                osend[s, q, :, n] = jnp.where(c == 0, high, low).astype(jnp.bfloat16)
+            out_copy(s, q).start()
+
+    def total(s, q):
+        return keep[s, q] + orecv[s, q].astype(jnp.float32)
 
     def collect(s):
-        out_copy(s).wait_recv()
-
-        @pl.when(s == 1)
-        def _():
-            for n in chunks(width, 512):
-                ssend[s, :, n] = total(s, n).astype(jnp.bfloat16)
-
-        @pl.when(s > 1)
-        def _():
-            sum_copy(s - 1, s).wait_recv()
-            for n in chunks(width, 512):
-                v = total(s, n) + srecv[s, :, n].astype(jnp.float32)
-                ssend[s, :, n] = v.astype(jnp.bfloat16)
-
-        sum_copy(s, (s + 1) % columns).start()
+        for q in range(PIECES):
+            out_copy(s, q).wait_recv()
+
+            @pl.when(s == 1)
+            def _():
+                ssend[s, q] = total(s, q).astype(jnp.bfloat16)
+
+            @pl.when(s > 1)
+            def _():
+                sum_copy(s - 1, s, q).wait_recv()
+                v = total(s, q) + srecv[s, q].astype(jnp.float32)
+                ssend[s, q] = v.astype(jnp.bfloat16)
+
+            sum_copy(s, (s + 1) % columns, q).start()
 
     def turn(t, carry):
         pl.when(t < columns)(lambda: front(t))
         pl.when((t >= 1) & (t < columns + 1))(lambda: middle(t - 1))
-        pl.when((t >= 2) & (t < columns + 2))(lambda: back(t - 2))
         pl.when(t >= 4)(lambda: collect(t - 3))
+
+        @pl.when(t == 3)
+        def _():
+            weights[-1].wait()
+
+        pl.when(t >= 3)(lambda: back(t - 2))
         return carry
 
-    lax.fori_loop(0, columns + 3, turn, 0)
-
-    out_copy(0).wait_recv()
-    sum_copy(last, 0).wait_recv()
-    for n in chunks(width, 512):
-        v = total(0, n) + srecv[0, :, n].astype(jnp.float32)
-        final[:, n] = v.astype(jnp.bfloat16)
-    give = remote(final, result, SUM, 0, 1, corner)
+    lax.fori_loop(0, columns + 2, turn, 0)
+    collect(last)
+    back(0)
     stay = pltpu.make_async_copy(final, result, local.at[0])
+    for q in range(PIECES):
+        out_copy(0, q).wait_recv()
+        sum_copy(last, 0, q).wait_recv()
+        v = total(0, q) + srecv[0, q].astype(jnp.float32)
+        final[:, q * span : (q + 1) * span] = v.astype(jnp.bfloat16)
+        pl.when(c != d)(lambda: give_copy(q).start())
 
     @pl.when(c == d)
     def _():
@@ -233,10 +281,8 @@
 
     @pl.when(c != d)
     def _():
-        give.start()
         move_tok.wait_send()
         move_meta.wait_send()
-        give.wait()
 
     def settle(s, carry):
         @pl.when(s < last)
@@ -247,63 +293,78 @@
         side_tok(s, c).wait_send()
         side_meta(s, c).wait_send()
         for e in range(held):
-            part_copy(s, e).wait_send()
+            for p in range(parts):
+                part_copy(s, e, p).wait_send()
         hidden_copy(s).wait_send()
-        out_copy(s).wait_send()
+        for q in range(PIECES):
+            out_copy(s, q).wait_send()
 
         @pl.when(s > 0)
         def _():
-            sum_copy(s, (s + 1) % columns).wait_send()
+            for q in range(PIECES):
+                sum_copy(s, (s + 1) % columns, q).wait_send()
 
         return carry
 
     lax.fori_loop(0, columns, settle, 0)
+
+    @pl.when(c != d)
+    def _():
+        for q in range(PIECES):
+            give_copy(q).wait()
 
 
 def near_layer(tokens, expert_ids, combine, gate, up, down, columns, experts, capacity):
     rows, width = tokens.shape
     held, depth, share = gate.shape
-    named = expert_ids[:, :, None] == jnp.arange(experts, dtype=jnp.int32)[None, None, :]
-    weight = jnp.sum(jnp.where(named, combine[:, :, None], 0.0), axis=1).T
-    chosen = jnp.any(named, axis=1).T
-    earlier = jnp.triu(jnp.ones((rows, rows), jnp.bfloat16), 1)
-    slot = jnp.dot(chosen.astype(jnp.bfloat16), earlier, preferred_element_type=jnp.float32)
-    slot = jnp.where(chosen, slot, -1.0)
-    meta = jnp.concatenate([slot, weight])
-    meta = jnp.concatenate([meta, meta], axis=1)
     bf16, f32 = jnp.bfloat16, jnp.float32
+    piece = 256 if share % 256 == 0 else 128
+    span = width // PIECES
+    parts = (held, share // piece, capacity, 2 * piece)
     return pl.pallas_call(
         functools.partial(layer_kernel, columns, experts, capacity),
         out_shape=jax.ShapeDtypeStruct((rows, width), bf16),
-        in_specs=[pl.BlockSpec(memory_space=pl.ANY)] * 5,
+        in_specs=[pl.BlockSpec(memory_space=pl.ANY)] * 6,
         out_specs=pl.BlockSpec(memory_space=pl.ANY),
         scratch_shapes=[
             pltpu.VMEM((columns, 2, rows, width), bf16),
             pltpu.VMEM((columns, 2, 2 * experts, 2 * rows), f32),
+            pltpu.VMEM((rows, width), bf16),
+            pltpu.VMEM((2 * experts, 2 * rows), f32),
+            pltpu.VMEM(expert_ids.shape, jnp.int32),
+            pltpu.VMEM(combine.shape, f32),
             pltpu.VMEM(gate.shape, bf16),
             pltpu.VMEM(up.shape, bf16),
             pltpu.VMEM(down.shape, bf16),
             pltpu.VMEM((held, 2 * capacity, width), bf16),
             pltpu.VMEM((columns, held, 2 * capacity, 2 * rows), bf16),
-            pltpu.VMEM((columns, held, capacity, 2 * share), f32),
-            pltpu.VMEM((columns, held, capacity, 2 * share), bf16),
-            pltpu.VMEM((columns, held, capacity, 2 * share), bf16),
+            pltpu.VMEM((columns, *parts), f32),
+            pltpu.VMEM((columns, *parts), bf16),
+            pltpu.VMEM((columns, *parts), bf16),
             pltpu.VMEM((columns, 2, held, capacity, share), bf16),
             pltpu.VMEM((2 * rows, held * share), bf16),
-            pltpu.VMEM((columns, rows, width), f32),
-            pltpu.VMEM((columns, rows, width), bf16),
-            pltpu.VMEM((columns, rows, width), bf16),
-            pltpu.VMEM((columns, rows, width), bf16),
-            pltpu.VMEM((columns, rows, width), bf16),
+            pltpu.VMEM((columns, PIECES, rows, span), f32),
+            pltpu.VMEM((columns, PIECES, rows, span), bf16),
+            pltpu.VMEM((columns, PIECES, rows, span), bf16),
+            pltpu.VMEM((columns, PIECES, rows, span), bf16),
+            pltpu.VMEM((columns, PIECES, rows, span), bf16),
             pltpu.VMEM((rows, width), bf16),
-            pltpu.SemaphoreType.DMA((KINDS, columns)),
-            pltpu.SemaphoreType.DMA((KINDS, columns)),
-            pltpu.SemaphoreType.DMA((2 * held + 3,)),
+            pltpu.SemaphoreType.DMA((5, columns)),
+            pltpu.SemaphoreType.DMA((5, columns)),
+            pltpu.SemaphoreType.DMA((held * parts[1], columns)),
+            pltpu.SemaphoreType.DMA((held * parts[1], columns)),
+            pltpu.SemaphoreType.DMA((PIECES, columns)),
+            pltpu.SemaphoreType.DMA((PIECES, columns)),
+            pltpu.SemaphoreType.DMA((PIECES, columns)),
+            pltpu.SemaphoreType.DMA((PIECES, columns)),
+            pltpu.SemaphoreType.DMA((PIECES,)),
+            pltpu.SemaphoreType.DMA((PIECES,)),
+            pltpu.SemaphoreType.DMA((2 * held + 4,)),
         ],
         compiler_params=pltpu.CompilerParams(
             collective_id=0, has_side_effects=True, vmem_limit_bytes=67043328
         ),
-    )(tokens, meta, gate, up, down)
+    )(tokens, expert_ids, combine, gate, up, down)
 
 
 def spread_tokens(tokens, groups, cores, width):
@@ -359,7 +420,7 @@
     capacity = min(rows, 3 * rows * top_count // (2 * experts))
     group = lax.axis_index("dp")
 
-    if groups == cores == 2 and columns % 2 == 0 and capacity % 16 == 0:
+    if groups == cores == 2 and columns % 2 == 0 and capacity % 16 == 0 and experts <= 128:
         return near_layer(
             tokens, expert_ids, combine, gate_weight, up_weight, down_weight,
             columns, experts, capacity,

time: 116 us -> 104 us (0.90)
  Pallas kernels: 112 us -> 98.9 us
  local copies, waits for them, and re-layouts: 1.67 us -> 4.42 us
  other arithmetic: 2.11 us -> 0 us
    pallas_call x1, Pallas kernels: 112 us -> 98.9 us  [near_layer(): pl.pallas_call(functools.partial(layer_kernel, columns, experts, capacity...]
    unnamed x1 -> x3, local copies, waits for them, and re-layouts: 1.67 us -> 4.42 us
where the time goes in v2:
time: 104 us; the launch traced here: 103 us
  Pallas kernels  98.9 us (95%)
  local copies, waits for them, and re-layouts  4.42 us (4%)
    pallas_call x1, Pallas kernels, near_layer(): pl.pallas_call(functools.partial(layer_kernel, columns, experts, capacity...  98.9 us
    unnamed x3, local copies, waits for them, and re-layouts  4.42 us

profile of v2, /device:TPU:1, one launch (start us, length us, event | category | flops | bytes accessed | tf_op | source)
XLA Modules:
  0.0 103.3 jit_solution(307806641942765502)
XLA Ops:
  0.0 1.4 %copy.7.ids = s32[64,8]{1,0:T(8,128)} copy(s32[64,8]{0,1:T(8,128)} %param.7) | data formatting | bytes 4096 | tf_op args[1]
  1.4 1.4 %copy.8.combine = f32[64,8]{1,0:T(8,128)} copy(f32[64,8]{0,1:T(8,128)} %param.8) | data formatting | bytes 4096 | tf_op args[2]
  2.8 98.9 %shard_map.64 = bf16[64,2048]{1,0:T(8,128)(2,1)} custom-call(bf16[64,2048]{1,0:T(8,128)(2,1)} %tokens.1, s32[64,8]{1,0:T(8,128)} %copy.7.ids, f32[64,8]{1,0:T(8,128)} %copy.8.combine, bf16[2,2048,768]{2,1,0:T(8,128)(2,1)} %gate.1, bf16[2,2048,768]{2,1,0:T(8,128)(2,1)} %up.1, bf16[2,768,2048]{2,1,0:T(8,128)(2,1)} %down.1), custom_call_target="tpu_custom_call" | custom-call | tf_op jit(solution)/shard_map/pallas_call | solution.py:324
  101.7 1.7 %copy.10 = bf16[64,2048]{1,0:T(8,128)(2,1)} copy(bf16[64,2048]{1,0:T(8,128)(2,1)} %shard_map.64) | data formatting | bytes 524288

commit v3 on v2

--- a/solution.py
+++ b/solution.py
@@ -8,7 +8,7 @@
 from jax.sharding import PartitionSpec as P
 
 MESH = pl.DeviceIdType.MESH
-RING, RING_META, SIDE, SIDE_META, HIDDEN = 0, 1, 2, 3, 4
+RING, RING_META, SIDE, SIDE_META, HIDDEN, PART, OUT, SUM, GIVE, MOVE, MOVE_META = range(11)
 PIECES = 4
 
 
@@ -18,27 +18,26 @@
 
 
 def routing_rows(ids, combine, experts):
-    rows, top = ids.shape
-    lane = lax.broadcasted_iota(jnp.int32, (rows, 128), 1)
-    weight = jnp.zeros((rows, 128), jnp.float32)
-    chosen = jnp.zeros((rows, 128), jnp.float32)
+    top, rows = ids.shape
+    number = lax.broadcasted_iota(jnp.int32, (experts, rows), 0)
+    weight = jnp.zeros((experts, rows), jnp.float32)
+    chosen = jnp.zeros((experts, rows), jnp.float32)
     for k in range(top):
-        same = lane == ids[:, k : k + 1]
-        weight = jnp.where(same, combine[:, k : k + 1], weight)
+        same = number == ids[k : k + 1]
+        weight = jnp.where(same, combine[k : k + 1], weight)
         chosen = jnp.where(same, 1.0, chosen)
-    before = lax.broadcasted_iota(jnp.int32, (rows, rows), 1)
-    before = (before < lax.broadcasted_iota(jnp.int32, (rows, rows), 0)).astype(jnp.bfloat16)
-    slot = jnp.dot(before, chosen.astype(jnp.bfloat16), preferred_element_type=jnp.float32)
+    before = lax.broadcasted_iota(jnp.int32, (rows, rows), 0)
+    before = (before < lax.broadcasted_iota(jnp.int32, (rows, rows), 1)).astype(jnp.bfloat16)
+    slot = jnp.dot(chosen.astype(jnp.bfloat16), before, preferred_element_type=jnp.float32)
     slot = jnp.where(chosen > 0, slot, -1.0)
-    return [jnp.concatenate([a, a]).T[:experts] for a in (slot, weight)]
+    return [jnp.concatenate([a, a], axis=1) for a in (slot, weight)]
 
 
 def layer_kernel(
     columns, experts, capacity,
     tokens, ids, combine, gate, up, down, result,
     tok, met, stage, mstage, idv, cov, wg, wu, wd, xs, pick, own, psend, precv, hid, dense,
-    keep, osend, orecv, ssend, srecv, final, sent, got, psent, pgot, osent, ogot, ssent, sgot,
-    fsent, fgot, local,
+    keep, osend, orecv, ssend, srecv, final, sent, got, ofine, sfine, local,
 ):
     d, i, c = lax.axis_index("dp"), lax.axis_index("expert"), lax.axis_index("etp")
     held, width, share = wg.shape
@@ -64,37 +63,47 @@
             device_id=device, device_id_type=MESH,
         )
 
-    def remote(src, dst, kind, s, r, device):
-        return copy(src, dst, sent.at[kind, s], got.at[kind, r], device)
+    def remote(src, dst, kind, r, device):
+        return copy(src, dst, sent.at[kind], got.at[kind, r], device)
 
     def ring_tok(s):
-        return remote(tok.at[s, c], tok.at[s + 1, c], RING, s, s + 1, ahead)
+        return remote(tok.at[s, c], tok.at[s + 1, c], RING, s + 1, ahead)
 
     def ring_meta(s):
-        return remote(met.at[s, c], met.at[s + 1, c], RING_META, s, s + 1, ahead)
+        return remote(met.at[s, c], met.at[s + 1, c], RING_META, s + 1, ahead)
 
     def side_tok(s, g):
-        return remote(tok.at[s, g], tok.at[s, g], SIDE, s, s, side)
+        return remote(tok.at[s, g], tok.at[s, g], SIDE, s, side)
 
     def side_meta(s, g):
-        return remote(met.at[s, g], met.at[s, g], SIDE_META, s, s, side)
-
-    def part_copy(s, e, p):
-        k = e * parts + p
-        return copy(psend.at[s, e, p], precv.at[s, e, p], psent.at[k, s], pgot.at[k, s], across)
+        return remote(met.at[s, g], met.at[s, g], SIDE_META, s, side)
+
+    def part_piece(s, e, p):
+        return remote(psend.at[s, e, p], precv.at[s, e, p], PART, s, across)
+
+    def part_all(s):
+        return remote(psend.at[s], precv.at[s], PART, s, across)
 
     def hidden_copy(s):
-        return remote(hid.at[s, 0], hid.at[s, 1], HIDDEN, s, s, across)
-
-    def out_copy(s, q):
-        return copy(osend.at[s, q], orecv.at[s, q], osent.at[q, s], ogot.at[q, s], side)
-
-    def sum_copy(s, after, q):
-        return copy(ssend.at[s, q], srecv.at[after, q], ssent.at[q, s], sgot.at[q, after], ahead)
-
-    def give_copy(q):
+        return remote(hid.at[s, 0], hid.at[s, 1], HIDDEN, s, across)
+
+    def out_piece(s, q, fine):
+        sem = ofine.at[0 if s == 0 else 1, q] if fine else got.at[OUT, s]
+        return copy(osend.at[s, q], orecv.at[s, q], sent.at[OUT], sem, side)
+
+    def out_all(s):
+        return remote(osend.at[s], orecv.at[s], OUT, s, side)
+
+    def sum_piece(s, after, q, fine):
+        sem = sfine.at[0 if after == 0 else 1, q] if fine else got.at[SUM, after]
+        return copy(ssend.at[s, q], srecv.at[after, q], sent.at[SUM], sem, ahead)
+
+    def sum_all(s, after):
+        return remote(ssend.at[s], srecv.at[after], SUM, after, ahead)
+
+    def give_piece(q):
         cols = pl.ds(q * span, span)
-        return copy(final.at[:, cols], result.at[:, cols], fsent.at[q], fgot.at[q], corner)
+        return remote(final.at[:, cols], result.at[:, cols], GIVE, 0, corner)
 
     weights = []
     for e in range(held):
@@ -106,10 +115,10 @@
     combine_copy = pltpu.make_async_copy(combine, cov, local.at[free + 1])
     keep_tok = pltpu.make_async_copy(tokens, tok.at[0, c], local.at[free + 2])
     stage_tok = pltpu.make_async_copy(tokens, stage, local.at[free + 2])
-    move_tok = remote(stage, tok.at[0, d], RING, last, 0, corner)
-    move_meta = remote(mstage, met.at[0, d], RING_META, last, 0, corner)
-    got_tok = remote(stage, tok.at[0, c], RING, last, 0, corner)
-    got_meta = remote(mstage, met.at[0, c], RING_META, last, 0, corner)
+    move_tok = copy(stage, tok.at[0, d], sent.at[MOVE], got.at[RING, 0], corner)
+    move_meta = copy(mstage, met.at[0, d], sent.at[MOVE_META], got.at[RING_META, 0], corner)
+    got_tok = copy(stage, tok.at[0, c], sent.at[MOVE], got.at[RING, 0], corner)
+    got_meta = copy(mstage, met.at[0, c], sent.at[MOVE_META], got.at[RING_META, 0], corner)
 
     barrier = pltpu.get_barrier_semaphore()
     for device in (ahead, behind, side, across, corner):
@@ -120,6 +129,13 @@
     pl.when(c != d)(lambda: stage_tok.start())
     for w in weights:
         w.start()
+    pl.semaphore_wait(barrier, 5)
+
+    @pl.when(c != d)
+    def _():
+        stage_tok.wait()
+        move_tok.start()
+
     ids_copy.wait()
     combine_copy.wait()
     slot_rows, weight_rows = routing_rows(idv[...], cov[...], experts)
@@ -134,13 +150,6 @@
     def _():
         mstage[:experts] = slot_rows
         mstage[experts:] = weight_rows
-        stage_tok.wait()
-
-    pl.semaphore_wait(barrier, 5)
-
-    @pl.when(c != d)
-    def _():
-        move_tok.start()
         move_meta.start()
         got_tok.wait_recv()
         got_meta.wait_recv()
@@ -194,15 +203,15 @@
                     to = slice(k * piece, (k + 1) * piece)
                     own[s, e, p, :, to] = v[:capacity]
                     psend[s, e, p, :, to] = v[capacity:].astype(jnp.bfloat16)
-                part_copy(s, e, p).start()
+                part_piece(s, e, p).start()
 
     def middle(s):
+        part_all(s).wait_recv()
         for e in range(held):
             hit = (slots == row_of(s, held * i + e)) & mine
             scale = row_of(s, experts + held * i + e)
             scale = jnp.sum(jnp.where(hit, scale, 0.0), axis=1, keepdims=True)
             for p in range(parts):
-                part_copy(s, e, p).wait_recv()
                 g = own[s, e, p, :, :piece] + precv[s, e, p, :, :piece].astype(jnp.float32)
                 u = own[s, e, p, :, piece:] + precv[s, e, p, :, piece:].astype(jnp.float32)
                 h = g / (1.0 + jnp.exp(-g)) * u * scale
@@ -211,7 +220,7 @@
         pl.when(s > 0)(lambda: hidden_copy(s).start())
         pl.when(s == last)(lambda: hidden_copy(0).start())
 
-    def back(s):
+    def back(s, fine):
         hidden_copy(s).wait_recv()
         for e in range(held):
             for n in chunks(share, 256):
@@ -230,14 +239,19 @@
                 low, high = v[:rows], v[rows:]
                 keep[s, q, :, n] = jnp.where(c == 0, low, high)
                 osend[s, q, :, n] = jnp.where(c == 0, high, low).astype(jnp.bfloat16)
-            out_copy(s, q).start()
+            out_piece(s, q, fine).start()
 
     def total(s, q):
         return keep[s, q] + orecv[s, q].astype(jnp.float32)
 
-    def collect(s):
+    def collect(s, fine_in, fine_out):
+        if not fine_in:
+            out_all(s).wait_recv()
+            pl.when(s > 1)(lambda: sum_all(s - 1, s).wait_recv())
         for q in range(PIECES):
-            out_copy(s, q).wait_recv()
+            if fine_in:
+                out_piece(s, q, True).wait_recv()
+                sum_piece(s - 1, s, q, True).wait_recv()
 
             @pl.when(s == 1)
             def _():
@@ -245,73 +259,56 @@
 
             @pl.when(s > 1)
             def _():
-                sum_copy(s - 1, s, q).wait_recv()
                 v = total(s, q) + srecv[s, q].astype(jnp.float32)
                 ssend[s, q] = v.astype(jnp.bfloat16)
 
-            sum_copy(s, (s + 1) % columns, q).start()
+            sum_piece(s, (s + 1) % columns, q, fine_out).start()
 
     def turn(t, carry):
         pl.when(t < columns)(lambda: front(t))
-        pl.when((t >= 1) & (t < columns + 1))(lambda: middle(t - 1))
-        pl.when(t >= 4)(lambda: collect(t - 3))
+        pl.when(t >= 1)(lambda: middle(t - 1))
+        pl.when(t >= 4)(lambda: collect(t - 3, False, False))
 
         @pl.when(t == 3)
         def _():
             weights[-1].wait()
 
-        pl.when(t >= 3)(lambda: back(t - 2))
+        pl.when(t >= 3)(lambda: back(t - 2, False))
         return carry
 
-    lax.fori_loop(0, columns + 2, turn, 0)
-    collect(last)
-    back(0)
-    stay = pltpu.make_async_copy(final, result, local.at[0])
+    lax.fori_loop(0, columns + 1, turn, 0)
+    collect(last - 1, False, True)
+    back(last, True)
+    collect(last, True, True)
+    back(0, True)
     for q in range(PIECES):
-        out_copy(0, q).wait_recv()
-        sum_copy(last, 0, q).wait_recv()
+        out_piece(0, q, True).wait_recv()
+        sum_piece(last, 0, q, True).wait_recv()
         v = total(0, q) + srecv[0, q].astype(jnp.float32)
-        final[:, q * span : (q + 1) * span] = v.astype(jnp.bfloat16)
-        pl.when(c != d)(lambda: give_copy(q).start())
-
-    @pl.when(c == d)
-    def _():
-        stay.start()
-        stay.wait()
+        v = v.astype(jnp.bfloat16)
+
+        @pl.when(c == d)
+        def _():
+            result[:, q * span : (q + 1) * span] = v
+
+        @pl.when(c != d)
+        def _():
+            final[:, q * span : (q + 1) * span] = v
+            give_piece(q).start()
+
+    early, late = pl.ds(0, last), pl.ds(1, last)
+    for src, kind in (
+        (tok.at[early, c], RING), (met.at[early, c], RING_META), (tok.at[:, c], SIDE),
+        (met.at[:, c], SIDE_META), (psend, PART), (hid.at[:, 0], HIDDEN), (osend, OUT),
+        (ssend.at[late], SUM),
+    ):
+        remote(src, src, kind, 0, ahead).wait_send()
 
     @pl.when(c != d)
     def _():
         move_tok.wait_send()
         move_meta.wait_send()
-
-    def settle(s, carry):
-        @pl.when(s < last)
-        def _():
-            ring_tok(s).wait_send()
-            ring_meta(s).wait_send()
-
-        side_tok(s, c).wait_send()
-        side_meta(s, c).wait_send()
-        for e in range(held):
-            for p in range(parts):
-                part_copy(s, e, p).wait_send()
-        hidden_copy(s).wait_send()
-        for q in range(PIECES):
-            out_copy(s, q).wait_send()
-
-        @pl.when(s > 0)
-        def _():
-            for q in range(PIECES):
-                sum_copy(s, (s + 1) % columns, q).wait_send()
-
-        return carry
-
-    lax.fori_loop(0, columns, settle, 0)
-
-    @pl.when(c != d)
-    def _():
-        for q in range(PIECES):
-            give_copy(q).wait()
+        remote(final, result, GIVE, 0, corner).wait()
 
 
 def near_layer(tokens, expert_ids, combine, gate, up, down, columns, experts, capacity):
@@ -323,16 +320,16 @@
     parts = (held, share // piece, capacity, 2 * piece)
     return pl.pallas_call(
         functools.partial(layer_kernel, columns, experts, capacity),
-        out_shape=jax.ShapeDtypeStruct((rows, width), bf16),
-        in_specs=[pl.BlockSpec(memory_space=pl.ANY)] * 6,
-        out_specs=pl.BlockSpec(memory_space=pl.ANY),
+        out_shape=pltpu.VMEM((rows, width), bf16),
+        in_specs=[pl.BlockSpec(memory_space=pltpu.HBM)] * 6,
+        out_specs=pl.BlockSpec(memory_space=pltpu.VMEM),
         scratch_shapes=[
             pltpu.VMEM((columns, 2, rows, width), bf16),
             pltpu.VMEM((columns, 2, 2 * experts, 2 * rows), f32),
             pltpu.VMEM((rows, width), bf16),
             pltpu.VMEM((2 * experts, 2 * rows), f32),
-            pltpu.VMEM(expert_ids.shape, jnp.int32),
-            pltpu.VMEM(combine.shape, f32),
+            pltpu.VMEM(expert_ids.shape[::-1], jnp.int32),
+            pltpu.VMEM(combine.shape[::-1], f32),
             pltpu.VMEM(gate.shape, bf16),
             pltpu.VMEM(up.shape, bf16),
             pltpu.VMEM(down.shape, bf16),
@@ -349,22 +346,16 @@
             pltpu.VMEM((columns, PIECES, rows, span), bf16),
             pltpu.VMEM((columns, PIECES, rows, span), bf16),
             pltpu.VMEM((rows, width), bf16),
-            pltpu.SemaphoreType.DMA((5, columns)),
-            pltpu.SemaphoreType.DMA((5, columns)),
-            pltpu.SemaphoreType.DMA((held * parts[1], columns)),
-            pltpu.SemaphoreType.DMA((held * parts[1], columns)),
-            pltpu.SemaphoreType.DMA((PIECES, columns)),
-            pltpu.SemaphoreType.DMA((PIECES, columns)),
-            pltpu.SemaphoreType.DMA((PIECES, columns)),
-            pltpu.SemaphoreType.DMA((PIECES, columns)),
-            pltpu.SemaphoreType.DMA((PIECES,)),
-            pltpu.SemaphoreType.DMA((PIECES,)),
+            pltpu.SemaphoreType.DMA((11,)),
+            pltpu.SemaphoreType.DMA((9, columns)),
+            pltpu.SemaphoreType.DMA((2, PIECES)),
+            pltpu.SemaphoreType.DMA((2, PIECES)),
             pltpu.SemaphoreType.DMA((2 * held + 4,)),
         ],
         compiler_params=pltpu.CompilerParams(
-            collective_id=0, has_side_effects=True, vmem_limit_bytes=67043328
+            collective_id=0, has_side_effects=True, vmem_limit_bytes=60 * 2**20
         ),
-    )(tokens, expert_ids, combine, gate, up, down)
+    )(tokens, expert_ids.T, combine.T, gate, up, down)
 
 
 def spread_tokens(tokens, groups, cores, width):

time: 104 us -> 99 us (0.952)
  local copies, waits for them, and re-layouts: 4.42 us -> 0.71 us
    unnamed x3 -> x1, local copies, waits for them, and re-layouts: 4.42 us -> 0.71 us
where the time goes in v3:
time: 99 us; the launch traced here: 98.8 us
  Pallas kernels  98.1 us (99%)
    pallas_call x1, Pallas kernels, near_layer(): pl.pallas_call(functools.partial(layer_kernel, columns, experts, capacity...  98.1 us

profile of v3, /device:TPU:1, one launch (start us, length us, event | category | flops | bytes accessed | tf_op | source)
XLA Modules:
  0.0 98.8 jit_solution(8687931079358170969)
XLA Ops:
  0.0 98.1 %shard_map.64 = bf16[64,2048]{1,0:T(8,128)(2,1)S(1)} custom-call(bf16[64,2048]{1,0:T(8,128)(2,1)} %tokens.1, s32[8,64]{1,0:T(8,128)} %bitcast.2, f32[8,64]{1,0:T(8,128)} %bitcast.3, bf16[2,2048,768]{2,1,0:T(8,128)(2,1)} %gate.1, bf16[2,2048,768]{2,1,0:T(8,128)(2,1)} %up.1, bf16[2,768,2048]{2,1,0:T(8,128)(2,1)} %down.1), custom_call_target="tpu_custom_call" | custom-call | tf_op jit(solution)/shard_map/pallas_call | solution.py:321
  98.1 0.7 copy.8

commit v4 on v3

--- a/solution.py
+++ b/solution.py
@@ -88,14 +88,14 @@
         return remote(hid.at[s, 0], hid.at[s, 1], HIDDEN, s, across)
 
     def out_piece(s, q, fine):
-        sem = ofine.at[0 if s == 0 else 1, q] if fine else got.at[OUT, s]
+        sem = ofine.at[(columns - s) % columns, q] if fine else got.at[OUT, s]
         return copy(osend.at[s, q], orecv.at[s, q], sent.at[OUT], sem, side)
 
     def out_all(s):
         return remote(osend.at[s], orecv.at[s], OUT, s, side)
 
     def sum_piece(s, after, q, fine):
-        sem = sfine.at[0 if after == 0 else 1, q] if fine else got.at[SUM, after]
+        sem = sfine.at[(columns - after) % columns, q] if fine else got.at[SUM, after]
         return copy(ssend.at[s, q], srecv.at[after, q], sent.at[SUM], sem, ahead)
 
     def sum_all(s, after):
@@ -129,40 +129,35 @@
     pl.when(c != d)(lambda: stage_tok.start())
     for w in weights:
         w.start()
+    ids_copy.wait()
+    combine_copy.wait()
+    slot_rows, weight_rows = routing_rows(idv[...], cov[...], experts)
+    mstage[:experts] = slot_rows
+    mstage[experts:] = weight_rows
+
+    @pl.when(c == d)
+    def _():
+        met[0, c, :experts] = slot_rows
+        met[0, c, experts:] = weight_rows
+
     pl.semaphore_wait(barrier, 5)
 
     @pl.when(c != d)
     def _():
         stage_tok.wait()
         move_tok.start()
-
-    ids_copy.wait()
-    combine_copy.wait()
-    slot_rows, weight_rows = routing_rows(idv[...], cov[...], experts)
-
-    @pl.when(c == d)
-    def _():
-        met[0, c, :experts] = slot_rows
-        met[0, c, experts:] = weight_rows
-        keep_tok.wait()
-
-    @pl.when(c != d)
-    def _():
-        mstage[:experts] = slot_rows
-        mstage[experts:] = weight_rows
         move_meta.start()
-        got_tok.wait_recv()
-        got_meta.wait_recv()
 
     lane = lax.broadcasted_iota(jnp.int32, (1, 2 * rows), 1)
     in_first = lane < rows
-    mine = (lane >= d * rows) & (lane < (d + 1) * rows)
+    kept = (lane < d * rows) | (lane >= (d + 1) * rows)
     slots = lax.broadcasted_iota(jnp.int32, (capacity, 2 * rows), 0).astype(jnp.float32)
+    slots_one = lax.broadcasted_iota(jnp.int32, (capacity, rows), 0).astype(jnp.float32)
 
     def row_of(s, r):
         return jnp.where(in_first, met[s, 0, pl.ds(r, 1), :], met[s, 1, pl.ds(r, 1), :])
 
-    def front(s):
+    def relay(s):
         @pl.when(s > 0)
         def _():
             ring_tok(s - 1).wait_recv()
@@ -176,18 +171,28 @@
             ring_tok(s).start()
             ring_meta(s).start()
 
+    def take(s):
         side_tok(s, 1 - c).wait_recv()
         side_meta(s, 1 - c).wait_recv()
+
+    def pack(s, g):
+        wide = []
         for e in range(held):
-            hit = slots == row_of(s, held * i + e)
-            pick[s, e, :capacity] = (hit & mine).astype(jnp.bfloat16)
-            pick[s, e, capacity:] = (hit & ~mine).astype(jnp.bfloat16)
-        picker = pick[s].reshape(held * 2 * capacity, 2 * rows)
+            row = met[s, g, pl.ds(held * i + e, 1), :]
+            wide.append(slots_one == row[:, :rows])
+        picker = jnp.concatenate(wide).astype(jnp.bfloat16)
         for n in chunks(width, 256):
-            packed = jnp.dot(
-                picker, tok[s, :, :, n].reshape(2 * rows, -1), preferred_element_type=jnp.float32
-            )
-            xs[:, :, n] = packed.astype(jnp.bfloat16).reshape(held, 2 * capacity, -1)
+            packed = jnp.dot(picker, tok[s, g, :, n], preferred_element_type=jnp.float32)
+            xs[:, :, n] = packed.astype(jnp.bfloat16).reshape(held, capacity, -1)
+
+    def gate_up(e, p, k):
+        w = (wg, wu)[k]
+        return jnp.dot(
+            xs[e], w[e, :, p * piece : (p + 1) * piece], preferred_element_type=jnp.float32
+        )
+
+    def send(s):
+        pack(s, d)
         for e in range(held):
             @pl.when(s == 0)
             def _():
@@ -195,20 +200,25 @@
                 weights[2 * e + 1].wait()
 
             for p in range(parts):
-                for k, w in enumerate((wg, wu)):
-                    v = jnp.dot(
-                        xs[e], w[e, :, p * piece : (p + 1) * piece],
-                        preferred_element_type=jnp.float32,
-                    )
+                for k in range(2):
                     to = slice(k * piece, (k + 1) * piece)
-                    own[s, e, p, :, to] = v[:capacity]
-                    psend[s, e, p, :, to] = v[capacity:].astype(jnp.bfloat16)
+                    psend[s, e, p, :, to] = gate_up(e, p, k).astype(jnp.bfloat16)
                 part_piece(s, e, p).start()
+
+    def keep_part(s):
+        pack(s, 1 - d)
+        for e in range(held):
+            hit = slots == row_of(s, held * i + e)
+            pick[s, e, :capacity] = (hit & kept).astype(jnp.bfloat16)
+            pick[s, e, capacity:] = (hit & ~kept).astype(jnp.bfloat16)
+            for p in range(parts):
+                for k in range(2):
+                    own[s, e, p, :, k * piece : (k + 1) * piece] = gate_up(e, p, k)
 
     def middle(s):
         part_all(s).wait_recv()
         for e in range(held):
-            hit = (slots == row_of(s, held * i + e)) & mine
+            hit = (slots == row_of(s, held * i + e)) & kept
             scale = row_of(s, experts + held * i + e)
             scale = jnp.sum(jnp.where(hit, scale, 0.0), axis=1, keepdims=True)
             for p in range(parts):
@@ -265,8 +275,29 @@
             sum_piece(s, (s + 1) % columns, q, fine_out).start()
 
     def turn(t, carry):
-        pl.when(t < columns)(lambda: front(t))
-        pl.when(t >= 1)(lambda: middle(t - 1))
+        @pl.when(c == d)
+        def _():
+            pl.when(t == 0)(lambda: keep_tok.wait())
+            relay(t)
+
+        pl.when(c != d)(lambda: take(t))
+        send(t)
+
+        @pl.when(c != d)
+        def _():
+            @pl.when(t == 0)
+            def _():
+                got_tok.wait_recv()
+                got_meta.wait_recv()
+
+            relay(t)
+
+        @pl.when(t >= 1)
+        def _():
+            pl.when(c == d)(lambda: take(t - 1))
+            keep_part(t - 1)
+            pl.when(t >= 2)(lambda: middle(t - 1))
+
         pl.when(t >= 4)(lambda: collect(t - 3, False, False))
 
         @pl.when(t == 3)
@@ -276,8 +307,14 @@
         pl.when(t >= 3)(lambda: back(t - 2, False))
         return carry
 
-    lax.fori_loop(0, columns + 1, turn, 0)
-    collect(last - 1, False, True)
+    lax.fori_loop(0, columns, turn, 0)
+    middle(0)
+    pl.when(c == d)(lambda: take(last))
+    keep_part(last)
+    middle(last)
+    collect(last - 2, False, True)
+    back(last - 1, True)
+    collect(last - 1, True, True)
     back(last, True)
     collect(last, True, True)
     back(0, True)
@@ -333,7 +370,7 @@
             pltpu.VMEM(gate.shape, bf16),
             pltpu.VMEM(up.shape, bf16),
             pltpu.VMEM(down.shape, bf16),
-            pltpu.VMEM((held, 2 * capacity, width), bf16),
+            pltpu.VMEM((held, capacity, width), bf16),
             pltpu.VMEM((columns, held, 2 * capacity, 2 * rows), bf16),
             pltpu.VMEM((columns, *parts), f32),
             pltpu.VMEM((columns, *parts), bf16),
@@ -348,8 +385,8 @@
             pltpu.VMEM((rows, width), bf16),
             pltpu.SemaphoreType.DMA((11,)),
             pltpu.SemaphoreType.DMA((9, columns)),
-            pltpu.SemaphoreType.DMA((2, PIECES)),
-            pltpu.SemaphoreType.DMA((2, PIECES)),
+            pltpu.SemaphoreType.DMA((3, PIECES)),
+            pltpu.SemaphoreType.DMA((3, PIECES)),
             pltpu.SemaphoreType.DMA((2 * held + 4,)),
         ],
         compiler_params=pltpu.CompilerParams(

time: 99 us -> 94.4 us (0.954)
  Pallas kernels: 98.1 us -> 93.5 us
    pallas_call x1, Pallas kernels: 98.1 us -> 93.5 us  [near_layer(): pl.pallas_call(functools.partial(layer_kernel, columns, experts, capacity...]
where the time goes in v4:
time: 94.4 us; the launch traced here: 94.2 us
  Pallas kernels  93.5 us (99%)
    pallas_call x1, Pallas kernels, near_layer(): pl.pallas_call(functools.partial(layer_kernel, columns, experts, capacity...  93.5 us

profile of v4, /device:TPU:1, one launch (start us, length us, event | category | flops | bytes accessed | tf_op | source)
XLA Modules:
  0.0 94.2 jit_solution(17685154117386658582)
XLA Ops:
  0.0 93.5 %shard_map.64 = bf16[64,2048]{1,0:T(8,128)(2,1)S(1)} custom-call(bf16[64,2048]{1,0:T(8,128)(2,1)} %tokens.1, s32[8,64]{1,0:T(8,128)} %bitcast.2, f32[8,64]{1,0:T(8,128)} %bitcast.3, bf16[2,2048,768]{2,1,0:T(8,128)(2,1)} %gate.1, bf16[2,2048,768]{2,1,0:T(8,128)(2,1)} %up.1, bf16[2,768,2048]{2,1,0:T(8,128)(2,1)} %down.1), custom_call_target="tpu_custom_call" | custom-call | tf_op jit(solution)/shard_map/pallas_call | solution.py:358
  93.5 0.7 copy.8

commit v5 on v4

--- a/solution.py
+++ b/solution.py
@@ -228,7 +228,7 @@
                 hid[s, 0, e, :, p * piece : (p + 1) * piece] = h.astype(jnp.bfloat16)
 
         pl.when(s > 0)(lambda: hidden_copy(s).start())
-        pl.when(s == last)(lambda: hidden_copy(0).start())
+        pl.when((s == last) & (c == 0))(lambda: hidden_copy(0).start())
 
     def back(s, fine):
         hidden_copy(s).wait_recv()
@@ -251,6 +251,32 @@
                 osend[s, q, :, n] = jnp.where(c == 0, high, low).astype(jnp.bfloat16)
             out_piece(s, q, fine).start()
 
+    def back_half(s, side_of):
+        g = d if side_of else 1 - d
+        away = (c + g) % 2
+        if side_of:
+            hidden_copy(s).wait_recv()
+        for e in range(held):
+            for n in chunks(share, 256):
+                spread = lax.dot_general(
+                    pick[s, e, side_of * capacity : (side_of + 1) * capacity],
+                    hid[s, side_of, e, :, n], (((0,), (0,)), ((), ())),
+                    preferred_element_type=jnp.float32,
+                )
+                dense[:, e * share + n.start : e * share + n.stop] = spread.astype(jnp.bfloat16)
+        for q in range(PIECES):
+            for n in chunks(span, 256):
+                v = jnp.dot(
+                    dense[pl.ds(pl.multiple_of(g * rows, rows), rows), :],
+                    wd[:, :, q * span + n.start : q * span + n.stop].reshape(held * share, -1),
+                    preferred_element_type=jnp.float32,
+                )
+
+                keep[s * (1 - away) + columns * away, q, :, n] = v
+                osend[s * away + columns * (1 - away), q, :, n] = v.astype(jnp.bfloat16)
+
+            pl.when(c != g)(lambda: out_piece(s, q, True).start())
+
     def total(s, q):
         return keep[s, q] + orecv[s, q].astype(jnp.float32)
 
@@ -282,6 +308,7 @@
 
         pl.when(c != d)(lambda: take(t))
         send(t)
+        pl.when(t >= 4)(lambda: collect(t - 3, False, False))
 
         @pl.when(c != d)
         def _():
@@ -298,8 +325,6 @@
             keep_part(t - 1)
             pl.when(t >= 2)(lambda: middle(t - 1))
 
-        pl.when(t >= 4)(lambda: collect(t - 3, False, False))
-
         @pl.when(t == 3)
         def _():
             weights[-1].wait()
@@ -311,32 +336,44 @@
     middle(0)
     pl.when(c == d)(lambda: take(last))
     keep_part(last)
+    back_half(last - 1, 0)
+    collect(last - 2, False, True)
+    back_half(0, 0)
     middle(last)
-    collect(last - 2, False, True)
-    back(last - 1, True)
-    collect(last - 1, True, True)
-    back(last, True)
-    collect(last, True, True)
-    back(0, True)
-    for q in range(PIECES):
+    back_half(last, 0)
+    pl.when(c != d)(lambda: collect(last - 1, True, True))
+    back_half(last - 1, 1)
+    pl.when(c == 1)(lambda: hidden_copy(0).start())
+    pl.when(c == d)(lambda: collect(last - 1, True, True))
+    pl.when(c != d)(lambda: collect(last, True, True))
+    back_half(last, 1)
+
+    def finish(q):
         out_piece(0, q, True).wait_recv()
         sum_piece(last, 0, q, True).wait_recv()
-        v = total(0, q) + srecv[0, q].astype(jnp.float32)
-        v = v.astype(jnp.bfloat16)
-
-        @pl.when(c == d)
-        def _():
-            result[:, q * span : (q + 1) * span] = v
-
-        @pl.when(c != d)
-        def _():
-            final[:, q * span : (q + 1) * span] = v
+        return (total(0, q) + srecv[0, q].astype(jnp.float32)).astype(jnp.bfloat16)
+
+    @pl.when(c == d)
+    def _():
+        collect(last, True, True)
+
+    @pl.when(c != d)
+    def _():
+        for q in range(PIECES):
+            final[:, q * span : (q + 1) * span] = finish(q)
             give_piece(q).start()
+
+    back_half(0, 1)
+
+    @pl.when(c == d)
+    def _():
+        for q in range(PIECES):
+            result[:, q * span : (q + 1) * span] = finish(q)
 
     early, late = pl.ds(0, last), pl.ds(1, last)
     for src, kind in (
         (tok.at[early, c], RING), (met.at[early, c], RING_META), (tok.at[:, c], SIDE),
-        (met.at[:, c], SIDE_META), (psend, PART), (hid.at[:, 0], HIDDEN), (osend, OUT),
+        (met.at[:, c], SIDE_META), (psend, PART), (hid.at[:, 0], HIDDEN), (osend.at[pl.ds(0, columns)], OUT),
         (ssend.at[late], SUM),
     ):
         remote(src, src, kind, 0, ahead).wait_send()
@@ -377,8 +414,8 @@
             pltpu.VMEM((columns, *parts), bf16),
             pltpu.VMEM((columns, 2, held, capacity, share), bf16),
             pltpu.VMEM((2 * rows, held * share), bf16),
-            pltpu.VMEM((columns, PIECES, rows, span), f32),
-            pltpu.VMEM((columns, PIECES, rows, span), bf16),
+            pltpu.VMEM((columns + 1, PIECES, rows, span), f32),
+            pltpu.VMEM((columns + 1, PIECES, rows, span), bf16),
             pltpu.VMEM((columns, PIECES, rows, span), bf16),
             pltpu.VMEM((columns, PIECES, rows, span), bf16),
             pltpu.VMEM((columns, PIECES, rows, span), bf16),

time: 94.4 us -> 94 us (level); the launches traced: 94.2 us -> 92.7 us
  Pallas kernels: 93.5 us -> 92 us
    pallas_call x1, Pallas kernels: 93.5 us -> 92 us  [near_layer(): pl.pallas_call(functools.partial(layer_kernel, columns, experts, capacity...]
where the time goes in v5:
time: 94 us; the launch traced here: 92.7 us
  Pallas kernels  92 us (98%)
    pallas_call x1, Pallas kernels, near_layer(): pl.pallas_call(functools.partial(layer_kernel, columns, experts, capacity...  92 us

profile of v5, /device:TPU:1, one launch (start us, length us, event | category | flops | bytes accessed | tf_op | source)
XLA Modules:
  0.0 92.7 jit_solution(15294104226820263100)
XLA Ops:
  0.0 92.0 %shard_map.64 = bf16[64,2048]{1,0:T(8,128)(2,1)S(1)} custom-call(bf16[64,2048]{1,0:T(8,128)(2,1)} %tokens.1, s32[8,64]{1,0:T(8,128)} %bitcast.2, f32[8,64]{1,0:T(8,128)} %bitcast.3, bf16[2,2048,768]{2,1,0:T(8,128)(2,1)} %gate.1, bf16[2,2048,768]{2,1,0:T(8,128)(2,1)} %up.1, bf16[2,768,2048]{2,1,0:T(8,128)(2,1)} %down.1), custom_call_target="tpu_custom_call" | custom-call | tf_op jit(solution)/shard_map/pallas_call | solution.py:395
  92.0 0.7 copy.8
